TPU v7x, 32 devices: a whole 2x2x4 slice. The times are simulated.
32 devices in a mesh: lat: 8 (over y, x, core), lon: 4 (over z).
Axes of the slice: x: 2, y: 2, z: 4, core: 2. Of those that a mesh axis runs over, the one named last changes fastest.
Arguments:
- inputs: bfloat16 [128, 384, 256], P('lat', 'lon'), may hold values from -6 to 6
- first_filter: bfloat16 [3, 3, 256, 256], replicated, may hold values from -0.125 to 0.125
- second_filter: bfloat16 [3, 3, 256, 256], replicated, may hold values from -0.125 to 0.125
- cotangent: bfloat16 [128, 384, 256], P('lat', 'lon'), may hold values from -30 to 30
Outputs:
- input_grad: bfloat16 [128, 384, 256], P('lat', 'lon')
- first_grad: float32 [3, 3, 256, 256], replicated
- second_grad: float32 [3, 3, 256, 256], replicated
All inputs are finite; a program needn't handle non-finite values.
Results may differ from a plain program's by a relative error of at most 0.0061.
Values may be sent and summed in bfloat16 or wider, within the bound.
A program may use at most 64 MiB of HBM per device.

v0:
```python
import jax
import jax.numpy as jnp
from jax import lax
from jax.sharding import PartitionSpec as P


def extended(block, sides, width):
    for axis, dim in sides:
        count = lax.axis_size(axis)
        forward = [(i, i + 1) for i in range(count - 1)]
        forward.append((count - 1, 0))
        backward = [(target, source) for source, target in forward]
        low = lax.ppermute(
            lax.slice_in_dim(block, block.shape[dim] - width, None, axis=dim), axis, forward
        )
        high = lax.ppermute(lax.slice_in_dim(block, 0, width, axis=dim), axis, backward)
        block = jnp.concatenate([low, block, high], axis=dim)
    return block


def mask_rows(padded, width):
    rows = padded.shape[0] - 2 * width
    position = lax.broadcasted_iota(jnp.int32, (padded.shape[0], 1, 1), 0)
    index = lax.axis_index("lat")
    count = lax.axis_size("lat")
    dropped = (position < width) & (index == 0) | (position >= rows + width) & (index == count - 1)
    return jnp.where(dropped, jnp.zeros((), padded.dtype), padded)


def extend(field):
    padded = extended(field, (("lat", 0), ("lon", 1)), 1)
    return mask_rows(padded, 1)


def conv_taps(padded, weight, rows, cols, flipped):
    total = jnp.zeros(
        (rows * cols, weight.shape[3] if not flipped else weight.shape[2]), jnp.float32
    )
    for first in range(3):
        for second in range(3):
            piece = padded[first : first + rows, second : second + cols, :].reshape(rows * cols, -1)
            if flipped:
                total = total + lax.dot_general(
                    piece,
                    weight[2 - first, 2 - second],
                    (((1,), (1,)), ((), ())),
                    preferred_element_type=jnp.float32,
                )
            else:
                total = total + jnp.dot(
                    piece, weight[first, second], preferred_element_type=jnp.float32
                )
    return total.reshape(rows, cols, -1)


def filter_grad(padded, delta, rows, cols):
    flat = delta.reshape(rows * cols, -1)
    taps = []
    for first in range(3):
        for second in range(3):
            piece = padded[first : first + rows, second : second + cols, :].reshape(rows * cols, -1)
            taps.append(
                lax.dot_general(
                    piece, flat, (((0,), (0,)), ((), ())), preferred_element_type=jnp.float32
                )
            )
    return jnp.stack(taps).reshape(3, 3, flat.shape[1], flat.shape[1])


def gelu_value(value):
    return value * 0.5 * (1.0 + jax.scipy.special.erf(value * 0.7071067811865476))


def gelu_slope(value):
    return (
        0.5 * (1.0 + jax.scipy.special.erf(value * 0.7071067811865476))
        + value * jnp.exp(-0.5 * value * value) * 0.3989422804014327
    )


def body(inputs, first_filter, second_filter, cotangent):
    rows, cols = (inputs.shape[0], inputs.shape[1])
    padded_in = extend(inputs)
    hidden_one = conv_taps(padded_in, first_filter, rows, cols, False)
    act = gelu_value(hidden_one).astype(jnp.bfloat16)
    padded_act = extend(act)
    hidden_two = conv_taps(padded_act, second_filter, rows, cols, False)
    delta_two = (cotangent.astype(jnp.float32) * gelu_slope(hidden_two)).astype(jnp.bfloat16)
    second_part = filter_grad(padded_act, delta_two, rows, cols)
    act_grad = conv_taps(extend(delta_two), second_filter, rows, cols, True)
    delta_one = (act_grad * gelu_slope(hidden_one)).astype(jnp.bfloat16)
    first_part = filter_grad(padded_in, delta_one, rows, cols)
    first_grad, second_grad = lax.psum((first_part, second_part), ("lat", "lon"))
    input_grad = conv_taps(extend(delta_one), first_filter, rows, cols, True).astype(jnp.bfloat16)
    return (input_grad, first_grad, second_grad)


def solution(mesh):
    in_specs = (P("lat", "lon", None), P(), P(), P("lat", "lon", None))
    out_specs = (P("lat", "lon", None), P(), P())
    return jax.shard_map(body, mesh=mesh, in_specs=in_specs, out_specs=out_specs, check_vma=False)
```

profile of v0, /device:TPU:0, one launch (start us, length us, event | category | flops | bytes accessed | tf_op | source)
XLA Modules:
  0.0 228.8 jit_solution(7460417335077282387)
XLA Ops:
  7.2 0.8 fusion.133
  8.0 0.5 collective-permute-start
  8.6 2.9 %collective-permute-start.1 = (bf16[1,96,256]{2,1,0:T(8,128)(2,1)S(1)}, bf16[1,96,256]{2,1,0:T(8,128)(2,1)S(1)}, u32[]{:S(2)}, u32[]{:S(2)}) collective-permute-start(bf16[1,96,256]{2,1,0:T(8,128)(2,1)S(1)} %get-tuple-element.55), channel_id=1, source_target_pairs={{4,0},{8,4},{12,8},{16,12},{20,16},{24,20},{28,24},{0,28},{5,1},{9... | collective-permute-start | bytes 147464 | tf_op jit(solution)/shard_map/ppermute | solution.py:16
  11.5 1.7 collective-permute-done
  13.2 1.2 constant_dynamic-update-slice_fusion.1
  14.5 4.4 %collective-permute-start.3 = (bf16[18,1,256]{2,1,0:T(2,128)(2,1)S(1)}, bf16[18,1,256]{2,1,0:T(2,128)(2,1)S(1)}, u32[]{:S(2)}, u32[]{:S(2)}) collective-permute-start(bf16[18,1,256]{2,1,0:T(2,128)(2,1)S(1)} %get-tuple-element.48), channel_id=1, source_target_pairs={{1,0},{2,1},{3,2},{0,3},{5,4},{6,5},{7,6},{4,7},{9,8},{10,9},{11,1... | collective-permute-start | bytes 27656 | tf_op jit(solution)/shard_map/ppermute | solution.py:16
  18.9 1.5 collective-permute-done.3
  20.3 4.1 %collective-permute-done.2 = bf16[18,1,256]{2,1,0:T(2,128)(2,1)S(1)} collective-permute-done((bf16[18,1,256]{2,1,0:T(2,128)(2,1)S(1)}, bf16[18,1,256]{2,1,0:T(2,128)(2,1)S(1)}, u32[]{:S(2)}, u32[]{:S(2)}) %collective-permute-start.2) | collective-permute-done | bytes 9248 | tf_op jit(solution)/shard_map/ppermute | solution.py:13
  24.4 0.6 maximum_select_fusion
  25.0 0.8 fusion.128
  25.9 0.4 copy-done.1
  30.0 0.5 collective-permute-start.4
  30.5 1.4 collective-permute-done.5
  31.9 2.6 %collective-permute-done.4 = bf16[1,96,256]{2,1,0:T(8,128)(2,1)S(1)} collective-permute-done((bf16[1,96,256]{2,1,0:T(8,128)(2,1)S(1)}, bf16[1,96,256]{2,1,0:T(8,128)(2,1)S(1)}, u32[]{:S(2)}, u32[]{:S(2)}) %collective-permute-start.4) | collective-permute-done | bytes 49184 | tf_op jit(solution)/shard_map/ppermute | solution.py:13
  34.8 1.8 collective-permute-start.6
  36.6 1.7 collective-permute-done.7
  38.4 2.0 collective-permute-done.6
  40.4 0.6 maximum_select_fusion.1
  40.9 1.1 fusion.127
  45.5 0.7 copy-done.5
  46.3 0.7 fusion.6
  47.0 0.4 fusion.21
  47.5 0.5 collective-permute-start.8
  48.0 0.4 fusion.20
  48.4 0.4 fusion.19
  48.8 0.4 fusion.18
  49.3 0.4 fusion.17
  49.7 0.4 fusion.16
  50.1 0.4 fusion.15
  50.5 0.4 fusion.14
  51.0 1.1 collective-permute-done.8
  52.2 2.0 collective-permute-start.10
  54.2 0.4 fusion.13
  54.7 1.3 collective-permute-done.11
  56.0 1.9 collective-permute-done.10
  57.8 0.6 maximum_select_fusion.2
  58.4 1.1 fusion.126
  63.1 0.7 fusion.12
  64.2 0.6 collective-permute-start.13
  64.8 0.4 fusion.29
  65.2 0.4 fusion.28
  65.7 0.4 fusion.27
  66.1 0.4 fusion.26
  66.5 0.4 fusion.25
  66.9 0.4 fusion.24
  67.4 0.4 fusion.23
  67.8 1.4 collective-permute-done.12
  69.3 2.0 collective-permute-start.14
  71.3 0.4 fusion.22
  71.8 1.4 copy-done.4
  73.2 2.0 collective-permute-done.14
  75.1 0.6 maximum_select_fusion.3
  75.7 1.1 fusion.125
  77.2 0.4 convolution_add_fusion.7
  77.6 0.4 convolution_add_fusion.6
  78.0 0.4 convolution_add_fusion.5
  78.4 0.4 convolution_add_fusion.4
  78.9 0.4 convolution_add_fusion.3
  79.3 0.4 convolution_add_fusion.2
  79.7 0.4 convolution_add_fusion.1
  80.1 1.3 fusion
  81.4 135.8 %all-reduce.3.cloned.1.call-done = (f32[3,3,256,256]{3,2,1,0:T(8,128)}, f32[3,3,256,256]{3,2,1,0:T(8,128)}) async-done(((f32[3,3,256,256]{3,2,1,0:T(8,128)}, f32[3,3,256,256]{3,2,1,0:T(8,128)}), (f32[3,3,256,256]{3,2,1,0:T(8,128)}, f32[3,3,256,256]{3,2,1,0:T(8,128)})) %all-reduce.3.cloned.1.call-update) | async-done | bytes 4718608 | tf_op jit(solution)/shard_map/psum | solution.py:93
  217.2 3.4 %copy.27 = f32[3,3,256,256]{3,2,1,0:T(8,128)} copy(f32[3,3,256,256]{3,2,1,0:T(8,128)} %get-tuple-element.58) | data formatting | bytes 4718592
  220.5 1.4 copy.28
  (62 shorter events, 12.2 us)
Async XLA Ops:
  7.2 210.0 %all-reduce.3.cloned.1.call-start = ((), (), s32[]{:S(2)}) async-start(), calls=%async_computation | async-start | bytes 9437184 | tf_op jit(solution)/shard_map/psum | solution.py:93
  8.0 5.2 %collective-permute-start = (bf16[1,96,256]{2,1,0:T(8,128)(2,1)S(1)}, bf16[1,96,256]{2,1,0:T(8,128)(2,1)S(1)}, u32[]{:S(2)}, u32[]{:S(2)}) collective-permute-start(bf16[1,96,256]{2,1,0:T(8,128)(2,1)S(1)} %get-tuple-element.56), channel_id=1, source_target_pairs={{0,4},{4,8},{8,12},{12,16},{16,20},{20,24},{24,28},{28,0},{1,5},{5... | collective-permute-start | bytes 147464 | tf_op jit(solution)/shard_map/ppermute | solution.py:13
  8.6 5.8 %collective-permute-start.1 = (bf16[1,96,256]{2,1,0:T(8,128)(2,1)S(1)}, bf16[1,96,256]{2,1,0:T(8,128)(2,1)S(1)}, u32[]{:S(2)}, u32[]{:S(2)}) collective-permute-start(bf16[1,96,256]{2,1,0:T(8,128)(2,1)S(1)} %get-tuple-element.55), channel_id=1, source_target_pairs={{4,0},{8,4},{12,8},{16,12},{20,16},{24,20},{28,24},{0,28},{5,1},{9... | collective-permute-start | bytes 147464 | tf_op jit(solution)/shard_map/ppermute | solution.py:16
  14.5 5.9 %collective-permute-start.3 = (bf16[18,1,256]{2,1,0:T(2,128)(2,1)S(1)}, bf16[18,1,256]{2,1,0:T(2,128)(2,1)S(1)}, u32[]{:S(2)}, u32[]{:S(2)}) collective-permute-start(bf16[18,1,256]{2,1,0:T(2,128)(2,1)S(1)} %get-tuple-element.48), channel_id=1, source_target_pairs={{1,0},{2,1},{3,2},{0,3},{5,4},{6,5},{7,6},{4,7},{9,8},{10,9},{11,1... | collective-permute-start | bytes 27656 | tf_op jit(solution)/shard_map/ppermute | solution.py:16
  18.9 5.6 %collective-permute-start.2 = (bf16[18,1,256]{2,1,0:T(2,128)(2,1)S(1)}, bf16[18,1,256]{2,1,0:T(2,128)(2,1)S(1)}, u32[]{:S(2)}, u32[]{:S(2)}) collective-permute-start(bf16[18,1,256]{2,1,0:T(2,128)(2,1)S(1)} %get-tuple-element.47), channel_id=1, source_target_pairs={{0,1},{1,2},{2,3},{3,0},{4,5},{5,6},{6,7},{7,4},{8,9},{9,10},{10,1... | collective-permute-start | bytes 27656 | tf_op jit(solution)/shard_map/ppermute | solution.py:13
  25.0 1.3 copy-start.1
  30.0 2.0 collective-permute-start.5
  30.0 4.5 %collective-permute-start.4 = (bf16[1,96,256]{2,1,0:T(8,128)(2,1)S(1)}, bf16[1,96,256]{2,1,0:T(8,128)(2,1)S(1)}, u32[]{:S(2)}, u32[]{:S(2)}) collective-permute-start(bf16[1,96,256]{2,1,0:T(8,128)(2,1)S(1)} %get-tuple-element.53), channel_id=1, source_target_pairs={{0,4},{4,8},{8,12},{12,16},{16,20},{20,24},{24,28},{28,0},{1,5},{5... | collective-permute-start | bytes 147464 | tf_op jit(solution)/shard_map/ppermute | solution.py:13
  34.5 3.8 %collective-permute-start.7 = (bf16[18,1,256]{2,1,0:T(2,128)(2,1)S(1)}, bf16[18,1,256]{2,1,0:T(2,128)(2,1)S(1)}, u32[]{:S(2)}, u32[]{:S(2)}) collective-permute-start(bf16[18,1,256]{2,1,0:T(2,128)(2,1)S(1)} %get-tuple-element.46), channel_id=1, source_target_pairs={{1,0},{2,1},{3,2},{0,3},{5,4},{6,5},{7,6},{4,7},{9,8},{10,9},{11,1... | collective-permute-start | bytes 27656 | tf_op jit(solution)/shard_map/ppermute | solution.py:16
  34.8 5.6 %collective-permute-start.6 = (bf16[18,1,256]{2,1,0:T(2,128)(2,1)S(1)}, bf16[18,1,256]{2,1,0:T(2,128)(2,1)S(1)}, u32[]{:S(2)}, u32[]{:S(2)}) collective-permute-start(bf16[18,1,256]{2,1,0:T(2,128)(2,1)S(1)} %get-tuple-element.45), channel_id=1, source_target_pairs={{0,1},{1,2},{2,3},{3,0},{4,5},{5,6},{6,7},{7,4},{8,9},{9,10},{10,1... | collective-permute-start | bytes 27656 | tf_op jit(solution)/shard_map/ppermute | solution.py:13
  40.9 1.3 copy-start
  45.1 1.1 copy-start.5
  47.4 3.6 %collective-permute-start.9 = (bf16[1,96,256]{2,1,0:T(8,128)(2,1)S(1)}, bf16[1,96,256]{2,1,0:T(8,128)(2,1)S(1)}, u32[]{:S(2)}, u32[]{:S(2)}) collective-permute-start(bf16[1,96,256]{2,1,0:T(8,128)(2,1)S(1)} %get-tuple-element.52), channel_id=1, source_target_pairs={{4,0},{8,4},{12,8},{16,12},{20,16},{24,20},{28,24},{0,28},{5,1},{9... | collective-permute-start | bytes 147464 | tf_op jit(solution)/shard_map/ppermute | solution.py:16
  47.5 4.6 %collective-permute-start.8 = (bf16[1,96,256]{2,1,0:T(8,128)(2,1)S(1)}, bf16[1,96,256]{2,1,0:T(8,128)(2,1)S(1)}, u32[]{:S(2)}, u32[]{:S(2)}) collective-permute-start(bf16[1,96,256]{2,1,0:T(8,128)(2,1)S(1)} %get-tuple-element.51), channel_id=1, source_target_pairs={{0,4},{4,8},{8,12},{12,16},{16,20},{20,24},{24,28},{28,0},{1,5},{5... | collective-permute-start | bytes 147464 | tf_op jit(solution)/shard_map/ppermute | solution.py:13
  52.2 3.8 %collective-permute-start.11 = (bf16[18,1,256]{2,1,0:T(2,128)(2,1)S(1)}, bf16[18,1,256]{2,1,0:T(2,128)(2,1)S(1)}, u32[]{:S(2)}, u32[]{:S(2)}) collective-permute-start(bf16[18,1,256]{2,1,0:T(2,128)(2,1)S(1)} %get-tuple-element.44), channel_id=1, source_target_pairs={{1,0},{2,1},{3,2},{0,3},{5,4},{6,5},{7,6},{4,7},{9,8},{10,9},{11,1... | collective-permute-start | bytes 27656 | tf_op jit(solution)/shard_map/ppermute | solution.py:16
  52.2 5.6 %collective-permute-start.10 = (bf16[18,1,256]{2,1,0:T(2,128)(2,1)S(1)}, bf16[18,1,256]{2,1,0:T(2,128)(2,1)S(1)}, u32[]{:S(2)}, u32[]{:S(2)}) collective-permute-start(bf16[18,1,256]{2,1,0:T(2,128)(2,1)S(1)} %get-tuple-element.43), channel_id=1, source_target_pairs={{0,1},{1,2},{2,3},{3,0},{4,5},{5,6},{6,7},{7,4},{8,9},{9,10},{10,1... | collective-permute-start | bytes 27656 | tf_op jit(solution)/shard_map/ppermute | solution.py:13
  54.7 4.8 %copy-start.3 = (f32[9,256,256]{2,1,0:T(8,128)}, f32[9,256,256]{2,1,0:T(8,128)S(1)}, u32[]{:S(2)}) copy-start(f32[9,256,256]{2,1,0:T(8,128)S(1)} %fusion.13) | copy-start | bytes 7077892
  64.2 3.6 %collective-permute-start.13 = (bf16[1,96,256]{2,1,0:T(8,128)(2,1)S(1)}, bf16[1,96,256]{2,1,0:T(8,128)(2,1)S(1)}, u32[]{:S(2)}, u32[]{:S(2)}) collective-permute-start(bf16[1,96,256]{2,1,0:T(8,128)(2,1)S(1)} %get-tuple-element.50), channel_id=1, source_target_pairs={{4,0},{8,4},{12,8},{16,12},{20,16},{24,20},{28,24},{0,28},{5,1},{9... | collective-permute-start | bytes 147464 | tf_op jit(solution)/shard_map/ppermute | solution.py:16
  64.8 4.4 %collective-permute-start.12 = (bf16[1,96,256]{2,1,0:T(8,128)(2,1)S(1)}, bf16[1,96,256]{2,1,0:T(8,128)(2,1)S(1)}, u32[]{:S(2)}, u32[]{:S(2)}) collective-permute-start(bf16[1,96,256]{2,1,0:T(8,128)(2,1)S(1)} %get-tuple-element.49), channel_id=1, source_target_pairs={{0,4},{4,8},{8,12},{12,16},{16,20},{20,24},{24,28},{28,0},{1,5},{5... | collective-permute-start | bytes 147464 | tf_op jit(solution)/shard_map/ppermute | solution.py:13
  69.2 3.9 %collective-permute-start.15 = (bf16[18,1,256]{2,1,0:T(2,128)(2,1)S(1)}, bf16[18,1,256]{2,1,0:T(2,128)(2,1)S(1)}, u32[]{:S(2)}, u32[]{:S(2)}) collective-permute-start(bf16[18,1,256]{2,1,0:T(2,128)(2,1)S(1)} %get-tuple-element.42), channel_id=1, source_target_pairs={{1,0},{2,1},{3,2},{0,3},{5,4},{6,5},{7,6},{4,7},{9,8},{10,9},{11,1... | collective-permute-start | bytes 27656 | tf_op jit(solution)/shard_map/ppermute | solution.py:16
  69.3 5.8 %collective-permute-start.14 = (bf16[18,1,256]{2,1,0:T(2,128)(2,1)S(1)}, bf16[18,1,256]{2,1,0:T(2,128)(2,1)S(1)}, u32[]{:S(2)}, u32[]{:S(2)}) collective-permute-start(bf16[18,1,256]{2,1,0:T(2,128)(2,1)S(1)} %get-tuple-element.41), channel_id=1, source_target_pairs={{0,1},{1,2},{2,3},{3,0},{4,5},{5,6},{6,7},{7,4},{8,9},{9,10},{10,1... | collective-permute-start | bytes 27656 | tf_op jit(solution)/shard_map/ppermute | solution.py:13
  71.7 1.4 copy-start.4
  217.2 3.4 %copy-start.2 = (f32[3,3,256,256]{3,2,1,0:T(8,128)S(1)}, f32[3,3,256,256]{3,2,1,0:T(8,128)}, u32[]{:S(2)}) copy-start(f32[3,3,256,256]{3,2,1,0:T(8,128)} %get-tuple-element.59) | copy-start | bytes 7077892
Sparse Core Ops, SparseCore 0:
  73.3 143.8 all-reduce.2
where the time goes:
time: 229 us
  waiting for transfers between devices  158 us (69%)
  matrix products  22.3 us (10%)
  starting transfers between devices  15.8 us (7%)
  between operations  14.6 us (6%)
  local copies, waits for them, and re-layouts  13.6 us (6%)
  other arithmetic  4.03 us (2%)
    psum x1, waiting for transfers between devices, body(): lax.psum((first_part, second_part), ('lat', 'lon'))  136 us
    ppermute x8, waiting for transfers between devices, extended(): lax.ppermute(lax.slice_in_dim(block, block.shape[dim] - width, None, axis...  16.7 us
    unnamed x16, local copies, waits for them, and re-layouts  8.77 us
    ppermute x8, starting transfers between devices, extended(): lax.ppermute(lax.slice_in_dim(block, 0, width, axis=dim), axis, backward)  8.4 us
    dot_general x18, matrix products, conv_taps(): lax.dot_general(piece, weight[2 - first, 2 - second], (((1,), (1,)), ((),...  8.18 us
    dot_general x18, matrix products, filter_grad(): lax.dot_general(piece, flat, (((0,), (0,)), ((), ())), preferred_element_...  7.54 us
    ppermute x8, starting transfers between devices, extended(): lax.ppermute(lax.slice_in_dim(block, block.shape[dim] - width, None, axis...  7.38 us
    dot_general x18, matrix products, conv_taps(): jnp.dot(piece, weight[first, second], preferred_element_type=jnp.float32)  6.59 us
  transfers between devices with their start and end apart: 17, of which 13 were waited for; matrix products, arithmetic and copies ran while one was open for 6% of the time, Pallas kernels for 0%

commit v1 on v0

--- a/solution.py
+++ b/solution.py
@@ -1,7 +1,245 @@
+import functools
+
 import jax
 import jax.numpy as jnp
 from jax import lax
+from jax.experimental import pallas as pl
+from jax.experimental.pallas import tpu as pltpu
 from jax.sharding import PartitionSpec as P
+
+MESH = pl.DeviceIdType.MESH
+PARTS = 3
+
+
+class Plan:
+    def __init__(self, mesh, rows):
+        self.lat, self.lon = mesh.shape["lat"], mesh.shape["lon"]
+        bits = self.lat.bit_length() - 1
+        if self.lat != 2**bits or bits < 1:
+            raise ValueError("lat size")
+        self.groups = [("lat", 2, 2**b) for b in range(1, bits)]
+        if self.lon > 1:
+            self.groups.append(("lon", self.lon, 1))
+        self.rows = rows
+        unit = 16 * (self.lat // 2) * self.lon
+        self.padded = -(-rows // unit) * unit
+        turn = max(1, len(self.groups) // PARTS)
+        self.orders = []
+        for p in range(PARTS):
+            s = (p * turn) % max(1, len(self.groups))
+            self.orders.append(self.groups[s:] + self.groups[:s])
+        self.peers = sum(size - 1 for _, size, _ in self.groups)
+        self.sems = 2 * (1 + self.peers)
+
+
+def member(group):
+    axis, size, stride = group
+    return (lax.axis_index(axis) // stride) % size
+
+
+def peer(group, k):
+    axis, size, stride = group
+    at = lax.axis_index(axis) + (k - member(group)) * stride
+    if axis == "lat":
+        return (at, lax.axis_index("lon"))
+    return (lax.axis_index("lat"), at)
+
+
+def partner():
+    lat = lax.axis_index("lat")
+    return (lat + 1 - 2 * (lat % 2), lax.axis_index("lon"))
+
+
+class Reduction:
+    def __init__(self, plan, index, grad, out, acc, sbuf, rbuf, send_sem, recv_sem):
+        self.plan, self.index, self.grad, self.out = plan, index, grad, out
+        self.acc, self.sbuf, self.rbuf = acc, sbuf, rbuf
+        self.send_sem, self.recv_sem = send_sem, recv_sem
+        self.core = lax.axis_index("lat") % 2
+        self.sent = []
+        self.pending = [[] for _ in range(PARTS)]
+        self.used = [0] * PARTS
+        self.base = [0] * PARTS
+        self.count = [plan.padded] * PARTS
+        self.offset = [0] * PARTS
+        self.steps = 2 * len(plan.groups) + 2
+
+    def send(self, p, src, dst, device):
+        slot = self.used[p]
+        self.used[p] += 1
+        copy = pltpu.make_async_remote_copy(
+            src_ref=src,
+            dst_ref=dst,
+            send_sem=self.send_sem.at[self.index, p, slot],
+            recv_sem=self.recv_sem.at[self.index, p, slot],
+            device_id=device,
+            device_id_type=MESH,
+        )
+        copy.start()
+        self.sent.append(copy)
+        self.pending[p].append(copy)
+
+    def arrive(self, p):
+        for copy in self.pending[p]:
+            copy.wait_recv()
+        self.pending[p] = []
+
+    def halves(self, p):
+        rows = self.plan.rows
+        block = self.grad[p * rows : (p + 1) * rows, :]
+        half = block.shape[1] // 2
+        low, high = block[:, :half], block[:, half:]
+        first = self.core == 0
+        return jnp.where(first, low, high), jnp.where(first, high, low)
+
+    def start(self):
+        plan = self.plan
+        for p in range(PARTS):
+            mine, other = self.halves(p)
+            if plan.padded > plan.rows:
+                shape = (plan.padded - plan.rows, mine.shape[1])
+                tail = pl.ds(plan.rows, plan.padded - plan.rows)
+                self.sbuf[self.index, p, tail, :] = jnp.zeros(shape, jnp.bfloat16)
+                self.acc[self.index, p, tail, :] = jnp.zeros(shape, jnp.float32)
+            self.sbuf[self.index, p, 0 : plan.rows, :] = other.astype(jnp.bfloat16)
+            self.acc[self.index, p, 0 : plan.rows, :] = mine
+            whole = pl.ds(0, plan.padded)
+            self.send(
+                p,
+                self.sbuf.at[self.index, p, whole],
+                self.rbuf.at[self.index, p, whole],
+                partner(),
+            )
+
+    def step(self, number):
+        for p in range(PARTS):
+            self.step_part(p, number)
+
+    def step_part(self, p, number):
+        order, i = self.plan.orders[p], self.index
+        depth = len(order)
+        self.arrive(p)
+        if number <= depth:
+            base, count = self.base[p], self.count[p]
+            if number == 0:
+                total = self.acc[i, p, 0:count, :]
+                total = total + self.rbuf[i, p, 0:count, :].astype(jnp.float32)
+                new_base = count
+            else:
+                group = order[number - 1]
+                size = group[1]
+                part = count // size
+                at = pl.multiple_of(member(group) * part, 16)
+                total = self.acc[i, p, pl.ds(pl.multiple_of(base + at, 16), part), :]
+                for t in range(size - 1):
+                    low = base + t * part
+                    total = total + self.rbuf[i, p, low : low + part, :].astype(jnp.float32)
+                new_base = base + count
+                count = part
+                self.offset[p] = self.offset[p] + at
+            self.base[p], self.count[p] = new_base, count
+            if number < depth:
+                self.acc[i, p, new_base : new_base + count, :] = total
+                self.sbuf[i, p, new_base : new_base + count, :] = total.astype(jnp.bfloat16)
+                group = order[number]
+                size = group[1]
+                part = count // size
+                for t in range(1, size):
+                    k = (member(group) + t) % size
+                    self.send(
+                        p,
+                        self.sbuf.at[i, p, pl.ds(pl.multiple_of(new_base + k * part, 16), part)],
+                        self.rbuf.at[i, p, pl.ds(new_base + (t - 1) * part, part)],
+                        peer(group, k),
+                    )
+            else:
+                at = pl.multiple_of(self.offset[p], 16)
+                self.out[self.core, p, pl.ds(at, count), :] = total.astype(jnp.bfloat16)
+                self.spread(p, order, depth)
+        else:
+            self.spread(p, order, 2 * depth - number)
+
+    def spread(self, p, order, level):
+        if level > 0:
+            group = order[level - 1]
+            span = pl.ds(pl.multiple_of(self.offset[p], 16), self.count[p])
+            block = self.out.at[self.core, p, span]
+            for t in range(1, group[1]):
+                k = (member(group) + t) % group[1]
+                self.send(p, block, block, peer(group, k))
+            self.offset[p] = self.offset[p] - member(group) * self.count[p]
+            self.count[p] *= group[1]
+        elif level == 0:
+            block = self.out.at[self.core, p]
+            self.send(p, block, block, partner())
+
+    def finish(self):
+        for copy in self.sent:
+            copy.wait_send()
+
+
+def greet(devices):
+    barrier = pltpu.get_barrier_semaphore()
+    for device in devices:
+        pl.semaphore_signal(barrier, inc=1, device_id=device, device_id_type=MESH)
+    pl.semaphore_wait(barrier, len(devices))
+
+
+def reduction_peers(plan):
+    found = [partner()]
+    for group in plan.groups:
+        for t in range(1, group[1]):
+            found.append(peer(group, (member(group) + t) % group[1]))
+    return found
+
+
+def sum_kernel(plan, first, second, out_a, out_b, acc, sbuf, rbuf, send_sem, recv_sem):
+    greet(reduction_peers(plan))
+    scratch = (acc, sbuf, rbuf, send_sem, recv_sem)
+    both = [
+        Reduction(plan, 0, first, out_a, *scratch),
+        Reduction(plan, 1, second, out_b, *scratch),
+    ]
+    for one in both:
+        one.start()
+    for number in range(both[0].steps):
+        for one in both:
+            one.step(number)
+    for one in both:
+        one.finish()
+
+
+def reduction_scratch(plan, half):
+    return [
+        pltpu.VMEM((2, PARTS, 3 * plan.padded, half), jnp.float32),
+        pltpu.VMEM((2, PARTS, 3 * plan.padded, half), jnp.bfloat16),
+        pltpu.VMEM((2, PARTS, 3 * plan.padded, half), jnp.bfloat16),
+        pltpu.SemaphoreType.DMA((2, PARTS, plan.sems)),
+        pltpu.SemaphoreType.DMA((2, PARTS, plan.sems)),
+    ]
+
+
+def unpacked(out, plan, shape):
+    value = out[:, :, : plan.rows, :].astype(jnp.float32)
+    return jnp.concatenate([value[0], value[1]], axis=-1).reshape(shape)
+
+
+def summed(mesh, first, second):
+    shape = first.shape
+    rows, half = shape[0] * shape[1] * shape[2] // PARTS, shape[3] // 2
+    plan = Plan(mesh, rows)
+    out = jax.ShapeDtypeStruct((2, PARTS, plan.padded, half), jnp.bfloat16)
+    a, b = pl.pallas_call(
+        functools.partial(sum_kernel, plan),
+        out_shape=(out, out),
+        in_specs=[pl.BlockSpec(memory_space=pltpu.VMEM)] * 2,
+        out_specs=[pl.BlockSpec(memory_space=pltpu.VMEM)] * 2,
+        scratch_shapes=reduction_scratch(plan, half),
+        compiler_params=pltpu.CompilerParams(
+            collective_id=0, has_side_effects=True, vmem_limit_bytes=60 * 2**20
+        ),
+    )(first.reshape(PARTS * rows, 2 * half), second.reshape(PARTS * rows, 2 * half))
+    return unpacked(a, plan, shape), unpacked(b, plan, shape)
 
 
 def extended(block, sides, width):
@@ -78,7 +316,7 @@
     )
 
 
-def body(inputs, first_filter, second_filter, cotangent):
+def body(mesh, inputs, first_filter, second_filter, cotangent):
     rows, cols = (inputs.shape[0], inputs.shape[1])
     padded_in = extend(inputs)
     hidden_one = conv_taps(padded_in, first_filter, rows, cols, False)
@@ -90,7 +328,7 @@
     act_grad = conv_taps(extend(delta_two), second_filter, rows, cols, True)
     delta_one = (act_grad * gelu_slope(hidden_one)).astype(jnp.bfloat16)
     first_part = filter_grad(padded_in, delta_one, rows, cols)
-    first_grad, second_grad = lax.psum((first_part, second_part), ("lat", "lon"))
+    first_grad, second_grad = summed(mesh, first_part, second_part)
     input_grad = conv_taps(extend(delta_one), first_filter, rows, cols, True).astype(jnp.bfloat16)
     return (input_grad, first_grad, second_grad)
 
@@ -98,4 +336,4 @@
 def solution(mesh):
     in_specs = (P("lat", "lon", None), P(), P(), P("lat", "lon", None))
     out_specs = (P("lat", "lon", None), P(), P())
-    return jax.shard_map(body, mesh=mesh, in_specs=in_specs, out_specs=out_specs, check_vma=False)
+    return jax.shard_map(functools.partial(body, mesh), mesh=mesh, in_specs=in_specs, out_specs=out_specs, check_vma=False)

time: 229 us -> 125 us (0.55)
  waiting for transfers between devices: 158 us -> 23.3 us
  Pallas kernels: 0 us -> 43.5 us
  between operations: 14.6 us -> 1.2 us
  other arithmetic: 4.03 us -> 7.18 us
  local copies, waits for them, and re-layouts: 13.6 us -> 10.9 us
    psum x1 -> x0, waiting for transfers between devices: 136 us -> none  [body(): lax.psum((first_part, second_part), ('lat', 'lon'))]
    pallas_call x0 -> x1, Pallas kernels: none -> 43.5 us  [summed(): pl.pallas_call(functools.partial(sum_kernel, plan), out_shape=(out, out),...]
    unnamed x16 -> x12, local copies, waits for them, and re-layouts: 8.77 us -> 3.99 us
    concatenate x0 -> x2, other arithmetic: none -> 3.15 us  [unpacked(): return jnp.concatenate([value[0], value[1]], axis=-1).reshape(shape)]
    ppermute x8, starting transfers between devices: 8.4 us -> 11 us  [extended(): lax.ppermute(lax.slice_in_dim(block, 0, width, axis=dim), axis, backward)]
  transfers between devices with their start and end apart: 17 -> 16, of which waited for: 13 -> 11; matrix products, arithmetic and copies ran while one was open for 6% -> 10% of each run, Pallas kernels for 0% -> 35%
where the time goes in v1:
time: 125 us
  Pallas kernels  43.5 us (35%)
  waiting for transfers between devices  23.3 us (19%)
  matrix products  22.3 us (18%)
  starting transfers between devices  16.3 us (13%)
  local copies, waits for them, and re-layouts  10.9 us (9%)
  other arithmetic  7.18 us (6%)
    pallas_call x1, Pallas kernels, summed(): pl.pallas_call(functools.partial(sum_kernel, plan), out_shape=(out, out),...  43.5 us
    ppermute x8, waiting for transfers between devices, extended(): lax.ppermute(lax.slice_in_dim(block, block.shape[dim] - width, None, axis...  17.4 us
    ppermute x8, starting transfers between devices, extended(): lax.ppermute(lax.slice_in_dim(block, 0, width, axis=dim), axis, backward)  11 us
    dot_general x18, matrix products, conv_taps(): lax.dot_general(piece, weight[2 - first, 2 - second], (((1,), (1,)), ((),...  8.18 us
    dot_general x18, matrix products, filter_grad(): lax.dot_general(piece, flat, (((0,), (0,)), ((), ())), preferred_element_...  7.52 us
    dot_general x18, matrix products, conv_taps(): jnp.dot(piece, weight[first, second], preferred_element_type=jnp.float32)  6.55 us
    ppermute x8, waiting for transfers between devices, extended(): lax.ppermute(lax.slice_in_dim(block, 0, width, axis=dim), axis, backward)  5.86 us
    ppermute x8, starting transfers between devices, extended(): lax.ppermute(lax.slice_in_dim(block, block.shape[dim] - width, None, axis...  5.31 us
  transfers between devices with their start and end apart: 16, of which 11 were waited for; matrix products, arithmetic and copies ran while one was open for 10% of the time, Pallas kernels for 35%

profile of v1, /device:TPU:0, one launch (start us, length us, event | category | flops | bytes accessed | tf_op | source)
XLA Modules:
  0.0 124.6 jit_solution(12830717127100727070)
XLA Ops:
  0.6 0.8 fusion.135
  1.5 0.5 collective-permute-start
  2.0 2.9 %collective-permute-start.1 = (bf16[1,96,256]{2,1,0:T(8,128)(2,1)S(1)}, bf16[1,96,256]{2,1,0:T(8,128)(2,1)S(1)}, u32[]{:S(2)}, u32[]{:S(2)}) collective-permute-start(bf16[1,96,256]{2,1,0:T(8,128)(2,1)S(1)} %get-tuple-element.61), channel_id=1, source_target_pairs={{4,0},{8,4},{12,8},{16,12},{20,16},{24,20},{28,24},{0,28},{5,1},{9... | collective-permute-start | bytes 147464 | tf_op jit(solution)/shard_map/ppermute | solution.py:254
  4.9 1.7 %collective-permute-done = bf16[1,96,256]{2,1,0:T(8,128)(2,1)S(1)} collective-permute-done((bf16[1,96,256]{2,1,0:T(8,128)(2,1)S(1)}, bf16[1,96,256]{2,1,0:T(8,128)(2,1)S(1)}, u32[]{:S(2)}, u32[]{:S(2)}) %collective-permute-start) | collective-permute-done | bytes 49184 | tf_op jit(solution)/shard_map/ppermute | solution.py:251
  6.6 1.2 constant_dynamic-update-slice_fusion.1
  7.9 4.4 %collective-permute-start.3 = (bf16[18,1,256]{2,1,0:T(2,128)(2,1)S(1)}, bf16[18,1,256]{2,1,0:T(2,128)(2,1)S(1)}, u32[]{:S(2)}, u32[]{:S(2)}) collective-permute-start(bf16[18,1,256]{2,1,0:T(2,128)(2,1)S(1)} %get-tuple-element.54), channel_id=1, source_target_pairs={{1,0},{2,1},{3,2},{0,3},{5,4},{6,5},{7,6},{4,7},{9,8},{10,9},{11,1... | collective-permute-start | bytes 27656 | tf_op jit(solution)/shard_map/ppermute | solution.py:254
  12.3 1.5 %collective-permute-done.3 = bf16[18,1,256]{2,1,0:T(2,128)(2,1)S(1)} collective-permute-done((bf16[18,1,256]{2,1,0:T(2,128)(2,1)S(1)}, bf16[18,1,256]{2,1,0:T(2,128)(2,1)S(1)}, u32[]{:S(2)}, u32[]{:S(2)}) %collective-permute-start.3) | collective-permute-done | bytes 9248 | tf_op jit(solution)/shard_map/ppermute | solution.py:254
  13.8 4.1 %collective-permute-done.2 = bf16[18,1,256]{2,1,0:T(2,128)(2,1)S(1)} collective-permute-done((bf16[18,1,256]{2,1,0:T(2,128)(2,1)S(1)}, bf16[18,1,256]{2,1,0:T(2,128)(2,1)S(1)}, u32[]{:S(2)}, u32[]{:S(2)}) %collective-permute-start.2) | collective-permute-done | bytes 9248 | tf_op jit(solution)/shard_map/ppermute | solution.py:251
  17.9 0.6 maximum_select_fusion
  18.5 0.8 fusion.130
  19.3 0.4 copy-done.1
  23.4 0.5 collective-permute-start.4
  23.9 1.4 %collective-permute-done.5 = bf16[1,96,256]{2,1,0:T(8,128)(2,1)S(1)} collective-permute-done((bf16[1,96,256]{2,1,0:T(8,128)(2,1)S(1)}, bf16[1,96,256]{2,1,0:T(8,128)(2,1)S(1)}, u32[]{:S(2)}, u32[]{:S(2)}) %collective-permute-start.5) | collective-permute-done | bytes 49184 | tf_op jit(solution)/shard_map/ppermute | solution.py:254
  25.3 2.6 %collective-permute-done.4 = bf16[1,96,256]{2,1,0:T(8,128)(2,1)S(1)} collective-permute-done((bf16[1,96,256]{2,1,0:T(8,128)(2,1)S(1)}, bf16[1,96,256]{2,1,0:T(8,128)(2,1)S(1)}, u32[]{:S(2)}, u32[]{:S(2)}) %collective-permute-start.4) | collective-permute-done | bytes 49184 | tf_op jit(solution)/shard_map/ppermute | solution.py:251
  28.2 1.8 %collective-permute-start.6 = (bf16[18,1,256]{2,1,0:T(2,128)(2,1)S(1)}, bf16[18,1,256]{2,1,0:T(2,128)(2,1)S(1)}, u32[]{:S(2)}, u32[]{:S(2)}) collective-permute-start(bf16[18,1,256]{2,1,0:T(2,128)(2,1)S(1)} %get-tuple-element.51), channel_id=1, source_target_pairs={{0,1},{1,2},{2,3},{3,0},{4,5},{5,6},{6,7},{7,4},{8,9},{9,10},{10,1... | collective-permute-start | bytes 27656 | tf_op jit(solution)/shard_map/ppermute | solution.py:251
  30.0 1.7 %collective-permute-done.7 = bf16[18,1,256]{2,1,0:T(2,128)(2,1)S(1)} collective-permute-done((bf16[18,1,256]{2,1,0:T(2,128)(2,1)S(1)}, bf16[18,1,256]{2,1,0:T(2,128)(2,1)S(1)}, u32[]{:S(2)}, u32[]{:S(2)}) %collective-permute-start.7) | collective-permute-done | bytes 9248 | tf_op jit(solution)/shard_map/ppermute | solution.py:254
  31.7 2.0 %collective-permute-done.6 = bf16[18,1,256]{2,1,0:T(2,128)(2,1)S(1)} collective-permute-done((bf16[18,1,256]{2,1,0:T(2,128)(2,1)S(1)}, bf16[18,1,256]{2,1,0:T(2,128)(2,1)S(1)}, u32[]{:S(2)}, u32[]{:S(2)}) %collective-permute-start.6) | collective-permute-done | bytes 9248 | tf_op jit(solution)/shard_map/ppermute | solution.py:251
  33.8 0.6 maximum_select_fusion.1
  34.4 1.1 fusion.129
  39.0 0.7 copy-done.4
  39.7 0.7 fusion.6
  40.9 0.5 collective-permute-start.8
  41.4 0.4 fusion.20
  41.8 0.4 fusion.19
  42.3 0.4 fusion.18
  42.7 0.4 fusion.17
  43.1 0.4 fusion.16
  43.6 0.4 fusion.15
  44.0 0.4 fusion.14
  44.4 1.1 collective-permute-done.8
  45.7 2.0 %collective-permute-start.10 = (bf16[18,1,256]{2,1,0:T(2,128)(2,1)S(1)}, bf16[18,1,256]{2,1,0:T(2,128)(2,1)S(1)}, u32[]{:S(2)}, u32[]{:S(2)}) collective-permute-start(bf16[18,1,256]{2,1,0:T(2,128)(2,1)S(1)} %get-tuple-element.49), channel_id=1, source_target_pairs={{0,1},{1,2},{2,3},{3,0},{4,5},{5,6},{6,7},{7,4},{8,9},{9,10},{10,1... | collective-permute-start | bytes 27656 | tf_op jit(solution)/shard_map/ppermute | solution.py:251
  47.7 0.4 fusion.13
  48.1 1.3 %collective-permute-done.11 = bf16[18,1,256]{2,1,0:T(2,128)(2,1)S(1)} collective-permute-done((bf16[18,1,256]{2,1,0:T(2,128)(2,1)S(1)}, bf16[18,1,256]{2,1,0:T(2,128)(2,1)S(1)}, u32[]{:S(2)}, u32[]{:S(2)}) %collective-permute-start.11) | collective-permute-done | bytes 9248 | tf_op jit(solution)/shard_map/ppermute | solution.py:254
  49.4 1.9 %collective-permute-done.10 = bf16[18,1,256]{2,1,0:T(2,128)(2,1)S(1)} collective-permute-done((bf16[18,1,256]{2,1,0:T(2,128)(2,1)S(1)}, bf16[18,1,256]{2,1,0:T(2,128)(2,1)S(1)}, u32[]{:S(2)}, u32[]{:S(2)}) %collective-permute-start.10) | collective-permute-done | bytes 9248 | tf_op jit(solution)/shard_map/ppermute | solution.py:251
  51.3 0.6 maximum_select_fusion.2
  51.8 1.1 fusion.128
  56.6 0.7 fusion.12
  57.6 0.6 collective-permute-start.13
  58.3 0.4 fusion.29
  58.7 0.4 fusion.28
  59.1 0.4 fusion.27
  59.5 0.4 fusion.26
  60.0 0.4 fusion.25
  60.4 0.4 fusion.24
  60.8 0.4 fusion.23
  61.2 0.4 fusion.22
  61.7 1.4 %copy-done.3 = f32[9,256,256]{2,1,0:T(8,128)} copy-done((f32[9,256,256]{2,1,0:T(8,128)}, f32[9,256,256]{2,1,0:T(8,128)S(1)}, u32[]{:S(2)}) %copy-start.3) | copy-done | bytes 2359320
  63.1 43.5 %shard_map.67 = (bf16[2,3,768,128]{3,2,1,0:T(8,128)(2,1)}, bf16[2,3,768,128]{3,2,1,0:T(8,128)(2,1)}) custom-call(f32[2304,256]{1,0:T(8,128)} %bitcast.325, f32[2304,256]{1,0:T(8,128)} %bitcast.324), custom_call_target="tpu_custom_call" | custom-call | tf_op jit(solution)/shard_map/pallas_call | solution.py:232
  106.6 2.0 %fusion.125 = (f32[1,3,768,128]{3,2,1,0:T(8,128)S(1)}, f32[1,3,768,128]{3,2,1,0:T(8,128)S(1)}, f32[1,3,768,128]{3,2,1,0:T(8,128)S(1)}, f32[1,3,768,128]{3,2,1,0:T(8,128)S(1)}) fusion(bf16[2,3,768,128]{3,2,1,0:T(8,128)(2,1)} %get-tuple-element.6, bf16[2,3,768,128]{3,2,1,0:T(8,128)(2,1)} %get-tuple-element.5), kind=kLoop, calls=%fused_computation.198 | loop fusion | bytes 9437184 | tf_op jit(solution)/shard_map/slice | solution.py:224
  108.6 1.6 %pad_maximum_fusion = f32[3,3,256,256]{3,2,1,0:T(8,128)} fusion(f32[3,3,256,128]{3,2,1,0:T(8,128)S(1)} %bitcast.286, f32[3,3,256,128]{3,2,1,0:T(8,128)S(1)} %bitcast.287), kind=kLoop, calls=%fused_computation.35 | loop fusion | flops 589824 | bytes 4718592 | tf_op jit(solution)/shard_map/concatenate | solution.py:224
  110.2 2.5 %collective-permute-start.15 = (bf16[18,1,256]{2,1,0:T(2,128)(2,1)S(1)}, bf16[18,1,256]{2,1,0:T(2,128)(2,1)S(1)}, u32[]{:S(2)}, u32[]{:S(2)}) collective-permute-start(bf16[18,1,256]{2,1,0:T(2,128)(2,1)S(1)} %get-tuple-element.48), channel_id=1, source_target_pairs={{1,0},{2,1},{3,2},{0,3},{5,4},{6,5},{7,6},{4,7},{9,8},{10,9},{11,1... | collective-permute-start | bytes 27656 | tf_op jit(solution)/shard_map/ppermute | solution.py:254
  112.8 1.6 %pad_maximum_fusion.1 = f32[3,3,256,256]{3,2,1,0:T(8,128)} fusion(f32[3,3,256,128]{3,2,1,0:T(8,128)S(1)} %bitcast.285, f32[3,3,256,128]{3,2,1,0:T(8,128)S(1)} %bitcast.284), kind=kLoop, calls=%fused_computation.36 | loop fusion | flops 589824 | bytes 4718592 | tf_op jit(solution)/shard_map/concatenate | solution.py:224
  114.4 4.0 %collective-permute-done.14 = bf16[18,1,256]{2,1,0:T(2,128)(2,1)S(1)} collective-permute-done((bf16[18,1,256]{2,1,0:T(2,128)(2,1)S(1)}, bf16[18,1,256]{2,1,0:T(2,128)(2,1)S(1)}, u32[]{:S(2)}, u32[]{:S(2)}) %collective-permute-start.14) | collective-permute-done | bytes 9248 | tf_op jit(solution)/shard_map/ppermute | solution.py:251
  118.3 0.6 maximum_select_fusion.3
  118.9 1.1 fusion.127
  120.0 0.4 fusion.51
  120.4 0.4 convolution_add_fusion.7
  120.8 0.4 convolution_add_fusion.6
  121.2 0.4 convolution_add_fusion.5
  121.6 0.4 convolution_add_fusion.4
  122.1 0.4 convolution_add_fusion.3
  122.5 0.4 convolution_add_fusion.2
  122.9 0.4 convolution_add_fusion.1
  123.3 1.3 %fusion = bf16[1536,256]{1,0:T(8,128)(2,1)} fusion(f32[1536,256]{1,0:T(8,128)S(1)} %convolution_add_fusion.1, bf16[1536,256]{1,0:T(8,128)(2,1)S(1)} %bitcast.292, bf16[3,3,256,256]{3,2,1,0:T(8,128)(2,1)S(1)} %copy-done.1), kind=kOutput, calls=%fused_computation.32 | convolution fusion | flops 202113024 | bytes 3276800 | tf_op jit(solution)/shard_map/dot_general | solution.py:281
  (59 shorter events, 12.1 us)
Async XLA Ops:
  1.5 5.2 %collective-permute-start = (bf16[1,96,256]{2,1,0:T(8,128)(2,1)S(1)}, bf16[1,96,256]{2,1,0:T(8,128)(2,1)S(1)}, u32[]{:S(2)}, u32[]{:S(2)}) collective-permute-start(bf16[1,96,256]{2,1,0:T(8,128)(2,1)S(1)} %get-tuple-element.62), channel_id=1, source_target_pairs={{0,4},{4,8},{8,12},{12,16},{16,20},{20,24},{24,28},{28,0},{1,5},{5... | collective-permute-start | bytes 147464 | tf_op jit(solution)/shard_map/ppermute | solution.py:251
  2.0 5.8 %collective-permute-start.1 = (bf16[1,96,256]{2,1,0:T(8,128)(2,1)S(1)}, bf16[1,96,256]{2,1,0:T(8,128)(2,1)S(1)}, u32[]{:S(2)}, u32[]{:S(2)}) collective-permute-start(bf16[1,96,256]{2,1,0:T(8,128)(2,1)S(1)} %get-tuple-element.61), channel_id=1, source_target_pairs={{4,0},{8,4},{12,8},{16,12},{20,16},{24,20},{28,24},{0,28},{5,1},{9... | collective-permute-start | bytes 147464 | tf_op jit(solution)/shard_map/ppermute | solution.py:254
  7.9 5.9 %collective-permute-start.3 = (bf16[18,1,256]{2,1,0:T(2,128)(2,1)S(1)}, bf16[18,1,256]{2,1,0:T(2,128)(2,1)S(1)}, u32[]{:S(2)}, u32[]{:S(2)}) collective-permute-start(bf16[18,1,256]{2,1,0:T(2,128)(2,1)S(1)} %get-tuple-element.54), channel_id=1, source_target_pairs={{1,0},{2,1},{3,2},{0,3},{5,4},{6,5},{7,6},{4,7},{9,8},{10,9},{11,1... | collective-permute-start | bytes 27656 | tf_op jit(solution)/shard_map/ppermute | solution.py:254
  12.3 5.6 %collective-permute-start.2 = (bf16[18,1,256]{2,1,0:T(2,128)(2,1)S(1)}, bf16[18,1,256]{2,1,0:T(2,128)(2,1)S(1)}, u32[]{:S(2)}, u32[]{:S(2)}) collective-permute-start(bf16[18,1,256]{2,1,0:T(2,128)(2,1)S(1)} %get-tuple-element.53), channel_id=1, source_target_pairs={{0,1},{1,2},{2,3},{3,0},{4,5},{5,6},{6,7},{7,4},{8,9},{9,10},{10,1... | collective-permute-start | bytes 27656 | tf_op jit(solution)/shard_map/ppermute | solution.py:251
  18.4 1.3 %copy-start.1 = (bf16[3,3,256,256]{3,2,1,0:T(8,128)(2,1)S(1)}, bf16[3,3,256,256]{3,2,1,0:T(8,128)(2,1)}, u32[]{:S(2)}) copy-start(bf16[3,3,256,256]{3,2,1,0:T(8,128)(2,1)} %param.5) | copy-start | bytes 3538948
  23.4 1.9 %collective-permute-start.5 = (bf16[1,96,256]{2,1,0:T(8,128)(2,1)S(1)}, bf16[1,96,256]{2,1,0:T(8,128)(2,1)S(1)}, u32[]{:S(2)}, u32[]{:S(2)}) collective-permute-start(bf16[1,96,256]{2,1,0:T(8,128)(2,1)S(1)} %get-tuple-element.60), channel_id=1, source_target_pairs={{4,0},{8,4},{12,8},{16,12},{20,16},{24,20},{28,24},{0,28},{5,1},{9... | collective-permute-start | bytes 147464 | tf_op jit(solution)/shard_map/ppermute | solution.py:254
  23.4 4.5 %collective-permute-start.4 = (bf16[1,96,256]{2,1,0:T(8,128)(2,1)S(1)}, bf16[1,96,256]{2,1,0:T(8,128)(2,1)S(1)}, u32[]{:S(2)}, u32[]{:S(2)}) collective-permute-start(bf16[1,96,256]{2,1,0:T(8,128)(2,1)S(1)} %get-tuple-element.59), channel_id=1, source_target_pairs={{0,4},{4,8},{8,12},{12,16},{16,20},{20,24},{24,28},{28,0},{1,5},{5... | collective-permute-start | bytes 147464 | tf_op jit(solution)/shard_map/ppermute | solution.py:251
  27.9 3.8 %collective-permute-start.7 = (bf16[18,1,256]{2,1,0:T(2,128)(2,1)S(1)}, bf16[18,1,256]{2,1,0:T(2,128)(2,1)S(1)}, u32[]{:S(2)}, u32[]{:S(2)}) collective-permute-start(bf16[18,1,256]{2,1,0:T(2,128)(2,1)S(1)} %get-tuple-element.52), channel_id=1, source_target_pairs={{1,0},{2,1},{3,2},{0,3},{5,4},{6,5},{7,6},{4,7},{9,8},{10,9},{11,1... | collective-permute-start | bytes 27656 | tf_op jit(solution)/shard_map/ppermute | solution.py:254
  28.2 5.6 %collective-permute-start.6 = (bf16[18,1,256]{2,1,0:T(2,128)(2,1)S(1)}, bf16[18,1,256]{2,1,0:T(2,128)(2,1)S(1)}, u32[]{:S(2)}, u32[]{:S(2)}) collective-permute-start(bf16[18,1,256]{2,1,0:T(2,128)(2,1)S(1)} %get-tuple-element.51), channel_id=1, source_target_pairs={{0,1},{1,2},{2,3},{3,0},{4,5},{5,6},{6,7},{7,4},{8,9},{9,10},{10,1... | collective-permute-start | bytes 27656 | tf_op jit(solution)/shard_map/ppermute | solution.py:251
  34.3 1.3 %copy-start = (bf16[3,3,256,256]{3,2,1,0:T(8,128)(2,1)S(1)}, bf16[3,3,256,256]{3,2,1,0:T(8,128)(2,1)}, u32[]{:S(2)}) copy-start(bf16[3,3,256,256]{3,2,1,0:T(8,128)(2,1)} %param.6) | copy-start | bytes 3538948
  38.6 1.1 copy-start.4
  40.8 3.6 %collective-permute-start.9 = (bf16[1,96,256]{2,1,0:T(8,128)(2,1)S(1)}, bf16[1,96,256]{2,1,0:T(8,128)(2,1)S(1)}, u32[]{:S(2)}, u32[]{:S(2)}) collective-permute-start(bf16[1,96,256]{2,1,0:T(8,128)(2,1)S(1)} %get-tuple-element.58), channel_id=1, source_target_pairs={{4,0},{8,4},{12,8},{16,12},{20,16},{24,20},{28,24},{0,28},{5,1},{9... | collective-permute-start | bytes 147464 | tf_op jit(solution)/shard_map/ppermute | solution.py:254
  40.9 4.6 %collective-permute-start.8 = (bf16[1,96,256]{2,1,0:T(8,128)(2,1)S(1)}, bf16[1,96,256]{2,1,0:T(8,128)(2,1)S(1)}, u32[]{:S(2)}, u32[]{:S(2)}) collective-permute-start(bf16[1,96,256]{2,1,0:T(8,128)(2,1)S(1)} %get-tuple-element.57), channel_id=1, source_target_pairs={{0,4},{4,8},{8,12},{12,16},{16,20},{20,24},{24,28},{28,0},{1,5},{5... | collective-permute-start | bytes 147464 | tf_op jit(solution)/shard_map/ppermute | solution.py:251
  45.6 3.8 %collective-permute-start.11 = (bf16[18,1,256]{2,1,0:T(2,128)(2,1)S(1)}, bf16[18,1,256]{2,1,0:T(2,128)(2,1)S(1)}, u32[]{:S(2)}, u32[]{:S(2)}) collective-permute-start(bf16[18,1,256]{2,1,0:T(2,128)(2,1)S(1)} %get-tuple-element.50), channel_id=1, source_target_pairs={{1,0},{2,1},{3,2},{0,3},{5,4},{6,5},{7,6},{4,7},{9,8},{10,9},{11,1... | collective-permute-start | bytes 27656 | tf_op jit(solution)/shard_map/ppermute | solution.py:254
  45.7 5.6 %collective-permute-start.10 = (bf16[18,1,256]{2,1,0:T(2,128)(2,1)S(1)}, bf16[18,1,256]{2,1,0:T(2,128)(2,1)S(1)}, u32[]{:S(2)}, u32[]{:S(2)}) collective-permute-start(bf16[18,1,256]{2,1,0:T(2,128)(2,1)S(1)} %get-tuple-element.49), channel_id=1, source_target_pairs={{0,1},{1,2},{2,3},{3,0},{4,5},{5,6},{6,7},{7,4},{8,9},{9,10},{10,1... | collective-permute-start | bytes 27656 | tf_op jit(solution)/shard_map/ppermute | solution.py:251
  48.1 4.8 %copy-start.2 = (f32[9,256,256]{2,1,0:T(8,128)}, f32[9,256,256]{2,1,0:T(8,128)S(1)}, u32[]{:S(2)}) copy-start(f32[9,256,256]{2,1,0:T(8,128)S(1)} %fusion.13) | copy-start | bytes 7077892
  57.6 52.6 %collective-permute-start.13 = (bf16[1,96,256]{2,1,0:T(8,128)(2,1)S(1)}, bf16[1,96,256]{2,1,0:T(8,128)(2,1)S(1)}, u32[]{:S(2)}, u32[]{:S(2)}) collective-permute-start(bf16[1,96,256]{2,1,0:T(8,128)(2,1)S(1)} %get-tuple-element.56), channel_id=1, source_target_pairs={{4,0},{8,4},{12,8},{16,12},{20,16},{24,20},{28,24},{0,28},{5,1},{9... | collective-permute-start | bytes 147464 | tf_op jit(solution)/shard_map/ppermute | solution.py:254
  58.3 52.0 %collective-permute-start.12 = (bf16[1,96,256]{2,1,0:T(8,128)(2,1)S(1)}, bf16[1,96,256]{2,1,0:T(8,128)(2,1)S(1)}, u32[]{:S(2)}, u32[]{:S(2)}) collective-permute-start(bf16[1,96,256]{2,1,0:T(8,128)(2,1)S(1)} %get-tuple-element.55), channel_id=1, source_target_pairs={{0,4},{4,8},{8,12},{12,16},{16,20},{20,24},{24,28},{28,0},{1,5},{5... | collective-permute-start | bytes 147464 | tf_op jit(solution)/shard_map/ppermute | solution.py:251
  61.7 1.4 %copy-start.3 = (f32[9,256,256]{2,1,0:T(8,128)}, f32[9,256,256]{2,1,0:T(8,128)S(1)}, u32[]{:S(2)}) copy-start(f32[9,256,256]{2,1,0:T(8,128)S(1)} %fusion.22) | copy-start | bytes 7077892
  110.2 4.1 %collective-permute-start.15 = (bf16[18,1,256]{2,1,0:T(2,128)(2,1)S(1)}, bf16[18,1,256]{2,1,0:T(2,128)(2,1)S(1)}, u32[]{:S(2)}, u32[]{:S(2)}) collective-permute-start(bf16[18,1,256]{2,1,0:T(2,128)(2,1)S(1)} %get-tuple-element.48), channel_id=1, source_target_pairs={{1,0},{2,1},{3,2},{0,3},{5,4},{6,5},{7,6},{4,7},{9,8},{10,9},{11,1... | collective-permute-start | bytes 27656 | tf_op jit(solution)/shard_map/ppermute | solution.py:254
  112.8 5.6 %collective-permute-start.14 = (bf16[18,1,256]{2,1,0:T(2,128)(2,1)S(1)}, bf16[18,1,256]{2,1,0:T(2,128)(2,1)S(1)}, u32[]{:S(2)}, u32[]{:S(2)}) collective-permute-start(bf16[18,1,256]{2,1,0:T(2,128)(2,1)S(1)} %get-tuple-element.47), channel_id=1, source_target_pairs={{0,1},{1,2},{2,3},{3,0},{4,5},{5,6},{6,7},{7,4},{8,9},{9,10},{10,1... | collective-permute-start | bytes 27656 | tf_op jit(solution)/shard_map/ppermute | solution.py:251

commit v2 on v1

--- a/solution.py
+++ b/solution.py
@@ -93,23 +93,26 @@
         return jnp.where(first, low, high), jnp.where(first, high, low)
 
     def start(self):
+        for p in range(PARTS):
+            self.start_part(p)
+
+    def start_part(self, p):
         plan = self.plan
-        for p in range(PARTS):
-            mine, other = self.halves(p)
-            if plan.padded > plan.rows:
-                shape = (plan.padded - plan.rows, mine.shape[1])
-                tail = pl.ds(plan.rows, plan.padded - plan.rows)
-                self.sbuf[self.index, p, tail, :] = jnp.zeros(shape, jnp.bfloat16)
-                self.acc[self.index, p, tail, :] = jnp.zeros(shape, jnp.float32)
-            self.sbuf[self.index, p, 0 : plan.rows, :] = other.astype(jnp.bfloat16)
-            self.acc[self.index, p, 0 : plan.rows, :] = mine
-            whole = pl.ds(0, plan.padded)
-            self.send(
-                p,
-                self.sbuf.at[self.index, p, whole],
-                self.rbuf.at[self.index, p, whole],
-                partner(),
-            )
+        mine, other = self.halves(p)
+        if plan.padded > plan.rows:
+            shape = (plan.padded - plan.rows, mine.shape[1])
+            tail = pl.ds(plan.rows, plan.padded - plan.rows)
+            self.sbuf[self.index, p, tail, :] = jnp.zeros(shape, jnp.bfloat16)
+            self.acc[self.index, p, tail, :] = jnp.zeros(shape, jnp.float32)
+        self.sbuf[self.index, p, 0 : plan.rows, :] = other.astype(jnp.bfloat16)
+        self.acc[self.index, p, 0 : plan.rows, :] = mine
+        whole = pl.ds(0, plan.padded)
+        self.send(
+            p,
+            self.sbuf.at[self.index, p, whole],
+            self.rbuf.at[self.index, p, whole],
+            partner(),
+        )
 
     def step(self, number):
         for p in range(PARTS):
@@ -193,19 +196,244 @@
     return found
 
 
-def sum_kernel(plan, first, second, out_a, out_b, acc, sbuf, rbuf, send_sem, recv_sem):
-    greet(reduction_peers(plan))
-    scratch = (acc, sbuf, rbuf, send_sem, recv_sem)
-    both = [
-        Reduction(plan, 0, first, out_a, *scratch),
-        Reduction(plan, 1, second, out_b, *scratch),
+def gelu_parts(value):
+    half = 0.5 * (1.0 + lax.erf(value * 0.7071067811865476))
+    slope = half + value * jnp.exp(-0.5 * value * value) * 0.3989422804014327
+    return value * half, slope
+
+
+class Halo:
+    def __init__(self, field, size, wide, edges, lines, got, gathered, corners, send_sem, recv_sem):
+        self.field, self.wide, self.edges, self.lines = field, wide, edges, lines
+        self.got, self.gathered, self.corners = got, gathered, corners
+        self.send_sem, self.recv_sem = send_sem, recv_sem
+        self.rows, self.cols, self.ch = size
+        self.copies = []
+
+    def put(self, row, values, count):
+        cols = self.cols
+        at = pl.multiple_of((row + 1) * cols, 16)
+        self.wide[self.field, pl.ds(at, count * cols), self.ch : 2 * self.ch] = values.astype(
+            jnp.bfloat16
+        )
+        for k in range(count):
+            self.edges[0, pl.ds(row + k, 1), :] = values[k * cols : k * cols + 1, :]
+            self.edges[1, pl.ds(row + k, 1), :] = values[(k + 1) * cols - 1 : (k + 1) * cols, :]
+
+    def center(self, start, count):
+        return self.wide.at[self.field, pl.ds(start, count), pl.ds(self.ch, self.ch)]
+
+    def send(self):
+        f, rows, cols = self.field, self.rows, self.cols
+        for side in range(2):
+            self.lines[f, side] = self.edges[side].astype(jnp.bfloat16)
+        devices = neighbours()
+        last = (rows + 1) * cols
+        top, bottom = cols, rows * cols
+        moves = [
+            (self.center(top, cols), self.center(last, cols)),
+            (self.center(bottom, cols), self.center(0, cols)),
+            (self.lines.at[f, 0], self.got.at[f, 1]),
+            (self.lines.at[f, 1], self.got.at[f, 0]),
+            (self.center(top, 16), self.corners.at[f, 3]),
+            (self.center(top + cols - 16, 16), self.corners.at[f, 2]),
+            (self.center(bottom, 16), self.corners.at[f, 1]),
+            (self.center(bottom + cols - 16, 16), self.corners.at[f, 0]),
+        ]
+        for slot, (src, dst) in enumerate(moves):
+            copy = pltpu.make_async_remote_copy(
+                src_ref=src,
+                dst_ref=dst,
+                send_sem=self.send_sem.at[f, slot],
+                recv_sem=self.recv_sem.at[f, slot],
+                device_id=devices[slot],
+                device_id_type=MESH,
+            )
+            copy.start()
+            self.copies.append(copy)
+
+    def shift_row(self, p):
+        f, cols, ch = self.field, self.cols, self.ch
+        at = pl.ds(pl.multiple_of(p * cols, 16), cols)
+        row = self.wide[f, at, ch : 2 * ch].astype(jnp.float32)
+        self.wide[f, at, 0:ch] = pltpu.roll(row, 1, 0).astype(jnp.bfloat16)
+        self.wide[f, at, 2 * ch : 3 * ch] = pltpu.roll(row, cols - 1, 0).astype(jnp.bfloat16)
+
+    def shift(self):
+        @pl.loop(1, self.rows + 1)
+        def _(p):
+            self.shift_row(p)
+
+    def receive(self):
+        f, rows, cols, ch = self.field, self.rows, self.cols, self.ch
+        for copy in self.copies:
+            copy.wait_recv()
+        lat, count = lax.axis_index("lat"), lax.axis_size("lat")
+        for p, dropped, pair in ((0, lat == 0, 0), (rows + 1, lat == count - 1, 2)):
+            keep = jnp.where(dropped, 0.0, 1.0)
+            at = pl.ds(p * cols, cols)
+            row = self.wide[f, at, ch : 2 * ch].astype(jnp.float32) * keep
+            self.wide[f, at, ch : 2 * ch] = row.astype(jnp.bfloat16)
+            left = self.corners[f, pair].astype(jnp.float32) * keep
+            right = self.corners[f, pair + 1].astype(jnp.float32) * keep
+            self.gathered[0, p : p + 1, :] = left[15:16, :]
+            self.gathered[1, p : p + 1, :] = right[0:1, :]
+            self.shift_row(p)
+        for side in range(2):
+            self.gathered[side, 1 : rows + 1, :] = self.got[f, side].astype(jnp.float32)
+        place = lax.broadcasted_iota(jnp.int32, (16, ch), 0)
+
+        @pl.loop(0, rows + 2)
+        def _(p):
+            low = pl.ds(pl.multiple_of(p * cols, 16), 16)
+            tile = self.wide[f, low, 0:ch].astype(jnp.float32)
+            edge = jnp.broadcast_to(self.gathered[0, pl.ds(p, 1), :], (16, ch))
+            self.wide[f, low, 0:ch] = jnp.where(place == 0, edge, tile).astype(jnp.bfloat16)
+            high = pl.ds(pl.multiple_of(p * cols + cols - 16, 16), 16)
+            tile = self.wide[f, high, 2 * ch : 3 * ch].astype(jnp.float32)
+            edge = jnp.broadcast_to(self.gathered[1, pl.ds(p, 1), :], (16, ch))
+            self.wide[f, high, 2 * ch : 3 * ch] = jnp.where(place == 15, edge, tile).astype(
+                jnp.bfloat16
+            )
+
+    def conv(self, row, count, weight):
+        total = None
+        for a in range(3):
+            at = pl.ds(pl.multiple_of((row + a) * self.cols, 16), count * self.cols)
+            part = jnp.dot(
+                self.wide[self.field, at, :], weight[a], preferred_element_type=jnp.float32
+            )
+            total = part if total is None else total + part
+        return total
+
+    def outer(self, delta, grad, a):
+        span = self.rows * self.cols
+        ch = self.ch
+        grad[a * 3 * ch : (a + 1) * 3 * ch, :] = lax.dot_general(
+            self.wide[self.field, pl.ds(a * self.cols, span), :],
+            delta.wide[delta.field, pl.ds(self.cols, span), ch : 2 * ch],
+            (((0,), (0,)), ((), ())),
+            preferred_element_type=jnp.float32,
+        )
+
+    def finish(self):
+        for copy in self.copies:
+            copy.wait_send()
+
+
+def neighbours():
+    lat, lon = lax.axis_index("lat"), lax.axis_index("lon")
+    lats, lons = lax.axis_size("lat"), lax.axis_size("lon")
+    up, down = (lat + lats - 1) % lats, (lat + 1) % lats
+    left, right = (lon + lons - 1) % lons, (lon + 1) % lons
+    return [
+        (up, lon),
+        (down, lon),
+        (lat, left),
+        (lat, right),
+        (up, left),
+        (up, right),
+        (down, left),
+        (down, right),
     ]
-    for one in both:
-        one.start()
-    for number in range(both[0].steps):
-        for one in both:
-            one.step(number)
-    for one in both:
+
+
+def main_kernel(plan, size, inputs, filter_one, filter_two, cotangent, *refs):
+    input_grad, out_one, out_two = refs[:3]
+    wide, edges, lines, got, gathered, corners, halo_send, halo_recv = refs[3:11]
+    slope_one, flip_one, flip_two, grad_one, grad_two = refs[11:16]
+    scratch = refs[16:]
+    rows, cols, ch = size
+    step = 4 if rows % 4 == 0 else 1
+    greet(neighbours() + reduction_peers(plan))
+    x, act, delta_two, delta_one = [
+        Halo(f, size, wide, edges, lines, got, gathered, corners, halo_send, halo_recv)
+        for f in range(4)
+    ]
+    sum_one = Reduction(plan, 0, grad_one, out_one, *scratch)
+    sum_two = Reduction(plan, 1, grad_two, out_two, *scratch)
+
+    def block(row):
+        return pl.ds(pl.multiple_of(row * cols, 16), step * cols)
+
+    @pl.loop(0, rows // step)
+    def _(c):
+        x.put(c * step, inputs[block(c * step), :].astype(jnp.float32), step)
+
+    x.send()
+    x.shift()
+    for source, target in ((filter_two, flip_two), (filter_one, flip_one)):
+
+        @pl.loop(0, 3)
+        def _(a):
+            for b in range(3):
+                tap = source[2 - a, (2 - b) * ch : (3 - b) * ch, :]
+                target[a, b * ch : (b + 1) * ch, :] = tap.T
+
+    x.receive()
+
+    @pl.loop(0, rows // step)
+    def _(c):
+        value, slope = gelu_parts(x.conv(c * step, step, filter_one))
+        slope_one[block(c * step), :] = slope
+        act.put(c * step, value, step)
+
+    act.send()
+    act.shift()
+    act.receive()
+
+    @pl.loop(0, rows // step)
+    def _(c):
+        _, slope = gelu_parts(act.conv(c * step, step, filter_two))
+        delta_two.put(c * step, cotangent[block(c * step), :].astype(jnp.float32) * slope, step)
+
+    delta_two.send()
+    delta_two.shift()
+    for a in range(3):
+        act.outer(delta_two, grad_two, a)
+        sum_two.start_part(a)
+    delta_two.receive()
+    sum_two.step(0)
+
+    @pl.loop(0, rows // step)
+    def _(c):
+        back = delta_two.conv(c * step, step, flip_two)
+        delta_one.put(c * step, back * slope_one[block(c * step), :], step)
+
+    delta_one.send()
+    delta_one.shift()
+    sum_two.step(1)
+    number = 2
+    for a in range(3):
+        x.outer(delta_one, grad_one, a)
+        sum_one.start_part(a)
+        if number < sum_two.steps:
+            sum_two.step(number)
+            number += 1
+    delta_one.receive()
+    done = 0
+    pieces = 2 if rows // step % 2 == 0 else 1
+    for piece in range(pieces):
+        sum_one.step(done)
+        done += 1
+        if number < sum_two.steps:
+            sum_two.step(number)
+            number += 1
+        first = piece * (rows // step // pieces)
+
+        @pl.loop(first, first + rows // step // pieces)
+        def _(c):
+            out = delta_one.conv(c * step, step, flip_one)
+            input_grad[block(c * step), :] = out.astype(jnp.bfloat16)
+
+    while done < sum_one.steps or number < sum_two.steps:
+        if done < sum_one.steps:
+            sum_one.step(done)
+            done += 1
+        if number < sum_two.steps:
+            sum_two.step(number)
+            number += 1
+    for one in (x, act, delta_two, delta_one, sum_one, sum_two):
         one.finish()
 
 
@@ -224,113 +452,50 @@
     return jnp.concatenate([value[0], value[1]], axis=-1).reshape(shape)
 
 
-def summed(mesh, first, second):
-    shape = first.shape
-    rows, half = shape[0] * shape[1] * shape[2] // PARTS, shape[3] // 2
-    plan = Plan(mesh, rows)
-    out = jax.ShapeDtypeStruct((2, PARTS, plan.padded, half), jnp.bfloat16)
-    a, b = pl.pallas_call(
-        functools.partial(sum_kernel, plan),
-        out_shape=(out, out),
-        in_specs=[pl.BlockSpec(memory_space=pltpu.VMEM)] * 2,
-        out_specs=[pl.BlockSpec(memory_space=pltpu.VMEM)] * 2,
-        scratch_shapes=reduction_scratch(plan, half),
+def body(mesh, inputs, first_filter, second_filter, cotangent):
+    rows, cols, ch = inputs.shape
+    plan = Plan(mesh, 3 * ch)
+    if plan.lon < 2 or cols % 16 or rows % 16:
+        raise ValueError("block size")
+    out = jax.ShapeDtypeStruct((2, PARTS, plan.padded, ch // 2), jnp.bfloat16)
+    vmem = pl.BlockSpec(memory_space=pltpu.VMEM)
+    flat = (rows * cols, ch)
+    input_grad, first, second = pl.pallas_call(
+        functools.partial(main_kernel, plan, (rows, cols, ch)),
+        out_shape=(jax.ShapeDtypeStruct(flat, jnp.bfloat16), out, out),
+        in_specs=[vmem] * 4,
+        out_specs=[vmem] * 3,
+        scratch_shapes=[
+            pltpu.VMEM((4, (rows + 2) * cols, 3 * ch), jnp.bfloat16),
+            pltpu.VMEM((2, rows, ch), jnp.float32),
+            pltpu.VMEM((4, 2, rows, ch), jnp.bfloat16),
+            pltpu.VMEM((4, 2, rows, ch), jnp.bfloat16),
+            pltpu.VMEM((2, rows + 8, ch), jnp.float32),
+            pltpu.VMEM((4, 4, 16, ch), jnp.bfloat16),
+            pltpu.SemaphoreType.DMA((4, 8)),
+            pltpu.SemaphoreType.DMA((4, 8)),
+            pltpu.VMEM(flat, jnp.float32),
+            pltpu.VMEM((3, 3 * ch, ch), jnp.bfloat16),
+            pltpu.VMEM((3, 3 * ch, ch), jnp.bfloat16),
+            pltpu.VMEM((9 * ch, ch), jnp.float32),
+            pltpu.VMEM((9 * ch, ch), jnp.float32),
+        ]
+        + reduction_scratch(plan, ch // 2),
         compiler_params=pltpu.CompilerParams(
-            collective_id=0, has_side_effects=True, vmem_limit_bytes=60 * 2**20
+            collective_id=0, has_side_effects=True, vmem_limit_bytes=62 * 2**20
         ),
-    )(first.reshape(PARTS * rows, 2 * half), second.reshape(PARTS * rows, 2 * half))
-    return unpacked(a, plan, shape), unpacked(b, plan, shape)
-
-
-def extended(block, sides, width):
-    for axis, dim in sides:
-        count = lax.axis_size(axis)
-        forward = [(i, i + 1) for i in range(count - 1)]
-        forward.append((count - 1, 0))
-        backward = [(target, source) for source, target in forward]
-        low = lax.ppermute(
-            lax.slice_in_dim(block, block.shape[dim] - width, None, axis=dim), axis, forward
-        )
-        high = lax.ppermute(lax.slice_in_dim(block, 0, width, axis=dim), axis, backward)
-        block = jnp.concatenate([low, block, high], axis=dim)
-    return block
-
-
-def mask_rows(padded, width):
-    rows = padded.shape[0] - 2 * width
-    position = lax.broadcasted_iota(jnp.int32, (padded.shape[0], 1, 1), 0)
-    index = lax.axis_index("lat")
-    count = lax.axis_size("lat")
-    dropped = (position < width) & (index == 0) | (position >= rows + width) & (index == count - 1)
-    return jnp.where(dropped, jnp.zeros((), padded.dtype), padded)
-
-
-def extend(field):
-    padded = extended(field, (("lat", 0), ("lon", 1)), 1)
-    return mask_rows(padded, 1)
-
-
-def conv_taps(padded, weight, rows, cols, flipped):
-    total = jnp.zeros(
-        (rows * cols, weight.shape[3] if not flipped else weight.shape[2]), jnp.float32
+    )(
+        inputs.reshape(flat),
+        first_filter.reshape(3, 3 * ch, ch),
+        second_filter.reshape(3, 3 * ch, ch),
+        cotangent.reshape(flat),
     )
-    for first in range(3):
-        for second in range(3):
-            piece = padded[first : first + rows, second : second + cols, :].reshape(rows * cols, -1)
-            if flipped:
-                total = total + lax.dot_general(
-                    piece,
-                    weight[2 - first, 2 - second],
-                    (((1,), (1,)), ((), ())),
-                    preferred_element_type=jnp.float32,
-                )
-            else:
-                total = total + jnp.dot(
-                    piece, weight[first, second], preferred_element_type=jnp.float32
-                )
-    return total.reshape(rows, cols, -1)
-
-
-def filter_grad(padded, delta, rows, cols):
-    flat = delta.reshape(rows * cols, -1)
-    taps = []
-    for first in range(3):
-        for second in range(3):
-            piece = padded[first : first + rows, second : second + cols, :].reshape(rows * cols, -1)
-            taps.append(
-                lax.dot_general(
-                    piece, flat, (((0,), (0,)), ((), ())), preferred_element_type=jnp.float32
-                )
-            )
-    return jnp.stack(taps).reshape(3, 3, flat.shape[1], flat.shape[1])
-
-
-def gelu_value(value):
-    return value * 0.5 * (1.0 + jax.scipy.special.erf(value * 0.7071067811865476))
-
-
-def gelu_slope(value):
+    shape = first_filter.shape
     return (
-        0.5 * (1.0 + jax.scipy.special.erf(value * 0.7071067811865476))
-        + value * jnp.exp(-0.5 * value * value) * 0.3989422804014327
+        input_grad.reshape(inputs.shape),
+        unpacked(first, plan, shape),
+        unpacked(second, plan, shape),
     )
-
-
-def body(mesh, inputs, first_filter, second_filter, cotangent):
-    rows, cols = (inputs.shape[0], inputs.shape[1])
-    padded_in = extend(inputs)
-    hidden_one = conv_taps(padded_in, first_filter, rows, cols, False)
-    act = gelu_value(hidden_one).astype(jnp.bfloat16)
-    padded_act = extend(act)
-    hidden_two = conv_taps(padded_act, second_filter, rows, cols, False)
-    delta_two = (cotangent.astype(jnp.float32) * gelu_slope(hidden_two)).astype(jnp.bfloat16)
-    second_part = filter_grad(padded_act, delta_two, rows, cols)
-    act_grad = conv_taps(extend(delta_two), second_filter, rows, cols, True)
-    delta_one = (act_grad * gelu_slope(hidden_one)).astype(jnp.bfloat16)
-    first_part = filter_grad(padded_in, delta_one, rows, cols)
-    first_grad, second_grad = summed(mesh, first_part, second_part)
-    input_grad = conv_taps(extend(delta_one), first_filter, rows, cols, True).astype(jnp.bfloat16)
-    return (input_grad, first_grad, second_grad)
 
 
 def solution(mesh):

time: 125 us -> 85.5 us (0.68)
  Pallas kernels: 43.5 us -> 78.6 us
  waiting for transfers between devices: 23.3 us -> 0 us
  matrix products: 22.3 us -> 0 us
  starting transfers between devices: 16.3 us -> 0 us
  local copies, waits for them, and re-layouts: 10.9 us -> 2.9 us
  other arithmetic: 7.18 us -> 3.15 us
    pallas_call x1, Pallas kernels: 43.5 us -> 78.6 us  [body(): pl.pallas_call(functools.partial(main_kernel, plan, (rows, cols, ch)), ou...]
    ppermute x16 -> x0, waiting for transfers between devices: 23.3 us -> none  [the longest x8 17.4 us: extended(): lax.ppermute(lax.slice_in_dim(block, block.shape[dim] - width, None, axis...]
    dot_general x54 -> x0, matrix products: 22.3 us -> none  [the longest x18 8.18 us: conv_taps(): lax.dot_general(piece, weight[2 - first, 2 - second], (((1,), (1,)), ((),...]
    ppermute x16 -> x0, starting transfers between devices: 16.3 us -> none  [the longest x8 11 us: extended(): lax.ppermute(lax.slice_in_dim(block, 0, width, axis=dim), axis, backward)]
    slice x9 -> x0, local copies, waits for them, and re-layouts: 4.87 us -> none  [the longest x4 3.98 us: conv_taps(): padded[first:first + rows, second:second + cols, :].reshape(rows * cols, -1)]
    unnamed x12 -> x3, local copies, waits for them, and re-layouts: 3.99 us -> 0.88 us
    select_n x4 -> x0, other arithmetic: 2.27 us -> none  [mask_rows(): return jnp.where(dropped, jnp.zeros((), padded.dtype), padded)]
    convert_element_type x3 -> x0, other arithmetic: 1.65 us -> none  [the longest x1 0.71 us: body(): (cotangent.astype(jnp.float32) * gelu_slope(hidden_two)).astype(jnp.bfloa...]
  transfers between devices with their start and end apart: 16 -> 0, of which waited for: 11 -> 0; matrix products, arithmetic and copies ran while one was open for 10% -> 0% of each run, Pallas kernels for 35% -> 0%
where the time goes in v2:
time: 85.5 us; the launch traced here: 85.3 us
  Pallas kernels  78.6 us (92%)
  other arithmetic  3.15 us (4%)
  local copies, waits for them, and re-layouts  2.9 us (3%)
    pallas_call x1, Pallas kernels, body(): pl.pallas_call(functools.partial(main_kernel, plan, (rows, cols, ch)), ou...  78.6 us
    concatenate x2, other arithmetic, unpacked(): return jnp.concatenate([value[0], value[1]], axis=-1).reshape(shape)  3.15 us
    slice x1, local copies, waits for them, and re-layouts, unpacked(): return jnp.concatenate([value[0], value[1]], axis=-1).reshape(shape)  2.02 us

profile of v2, /device:TPU:0, one launch (start us, length us, event | category | flops | bytes accessed | tf_op | source)
XLA Modules:
  0.0 85.3 jit_solution(10022577487194503025)
XLA Ops:
  0.6 78.6 %shard_map.67 = (bf16[1536,256]{1,0:T(8,128)(2,1)}, bf16[2,3,768,128]{3,2,1,0:T(8,128)(2,1)}, bf16[2,3,768,128]{3,2,1,0:T(8,128)(2,1)}) custom-call(bf16[1536,256]{1,0:T(8,128)(2,1)} %bitcast.16, bf16[3,768,256]{2,1,0:T(8,128)(2,1)} %bitcast.13, bf16[3,768,256]{2,1,0:T(8,128)(2,1)} %bitcast.14, bf16[1536,256]{1,0:T(8,128)(2,1)} %bitcast.17), custom_call_target="tpu_custom_call" | custom-call | tf_op jit(solution)/shard_map/pallas_call | solution.py:463
  79.3 2.0 %fusion = (f32[1,3,768,128]{3,2,1,0:T(8,128)S(1)}, f32[1,3,768,128]{3,2,1,0:T(8,128)S(1)}, f32[1,3,768,128]{3,2,1,0:T(8,128)S(1)}, f32[1,3,768,128]{3,2,1,0:T(8,128)S(1)}) fusion(bf16[2,3,768,128]{3,2,1,0:T(8,128)(2,1)} %get-tuple-element.8, bf16[2,3,768,128]{3,2,1,0:T(8,128)(2,1)} %get-tuple-element.7), kind=kLoop, calls=%fused_computation.2 | loop fusion | bytes 9437184 | tf_op jit(solution)/shard_map/slice | solution.py:452
  81.3 1.6 %pad_maximum_fusion.1 = f32[3,3,256,256]{3,2,1,0:T(8,128)} fusion(f32[3,3,256,128]{3,2,1,0:T(8,128)S(1)} %bitcast.12, f32[3,3,256,128]{3,2,1,0:T(8,128)S(1)} %bitcast.11), kind=kLoop, calls=%fused_computation.1 | loop fusion | flops 589824 | bytes 4718592 | tf_op jit(solution)/shard_map/concatenate | solution.py:452
  82.9 0.0 copy-start
  82.9 1.6 %pad_maximum_fusion = f32[3,3,256,256]{3,2,1,0:T(8,128)} fusion(f32[3,3,256,128]{3,2,1,0:T(8,128)S(1)} %bitcast.9, f32[3,3,256,128]{3,2,1,0:T(8,128)S(1)} %bitcast.10), kind=kLoop, calls=%fused_computation | loop fusion | flops 589824 | bytes 4718592 | tf_op jit(solution)/shard_map/concatenate | solution.py:452
  84.4 0.0 copy-done
  84.5 0.9 %copy.8 = bf16[16,96,256]{2,1,0:T(8,128)(2,1)} copy(bf16[16,96,256]{2,1,0:T(8,128)(2,1)S(1)} %bitcast.15) | data formatting | bytes 1572864
Async XLA Ops:
  82.9 1.6 %copy-start = (bf16[1536,256]{1,0:T(8,128)(2,1)S(1)}, bf16[1536,256]{1,0:T(8,128)(2,1)}, u32[]{:S(2)}) copy-start(bf16[1536,256]{1,0:T(8,128)(2,1)} %get-tuple-element.6) | copy-start | bytes 2359300

commit v3 on v2

--- a/solution.py
+++ b/solution.py
@@ -14,20 +14,14 @@
 class Plan:
     def __init__(self, mesh, rows):
         self.lat, self.lon = mesh.shape["lat"], mesh.shape["lon"]
-        bits = self.lat.bit_length() - 1
-        if self.lat != 2**bits or bits < 1:
-            raise ValueError("lat size")
-        self.groups = [("lat", 2, 2**b) for b in range(1, bits)]
-        if self.lon > 1:
-            self.groups.append(("lon", self.lon, 1))
+        if self.lat % 2 or self.lat < 4 or self.lon < 2:
+            raise ValueError("mesh size")
+        across, along = ("lat", self.lat // 2, 2), ("lon", self.lon, 1)
+        self.groups = [across, along]
+        self.orders = [[across, along], [across, along], [along, across]]
         self.rows = rows
         unit = 16 * (self.lat // 2) * self.lon
         self.padded = -(-rows // unit) * unit
-        turn = max(1, len(self.groups) // PARTS)
-        self.orders = []
-        for p in range(PARTS):
-            s = (p * turn) % max(1, len(self.groups))
-            self.orders.append(self.groups[s:] + self.groups[:s])
         self.peers = sum(size - 1 for _, size, _ in self.groups)
         self.sems = 2 * (1 + self.peers)
 
@@ -157,23 +151,27 @@
                     )
             else:
                 at = pl.multiple_of(self.offset[p], 16)
-                self.out[self.core, p, pl.ds(at, count), :] = total.astype(jnp.bfloat16)
+                self.out[p, pl.ds(at, count), self.lanes()] = total.astype(jnp.bfloat16)
                 self.spread(p, order, depth)
         else:
             self.spread(p, order, 2 * depth - number)
+
+    def lanes(self):
+        half = self.out.shape[2] // 2
+        return pl.ds(pl.multiple_of(self.core * half, half), half)
 
     def spread(self, p, order, level):
         if level > 0:
             group = order[level - 1]
             span = pl.ds(pl.multiple_of(self.offset[p], 16), self.count[p])
-            block = self.out.at[self.core, p, span]
+            block = self.out.at[p, span, self.lanes()]
             for t in range(1, group[1]):
                 k = (member(group) + t) % group[1]
                 self.send(p, block, block, peer(group, k))
             self.offset[p] = self.offset[p] - member(group) * self.count[p]
             self.count[p] *= group[1]
         elif level == 0:
-            block = self.out.at[self.core, p]
+            block = self.out.at[p, pl.ds(0, self.plan.padded), self.lanes()]
             self.send(p, block, block, partner())
 
     def finish(self):
@@ -297,14 +295,13 @@
             )
 
     def conv(self, row, count, weight):
-        total = None
+        pieces = []
         for a in range(3):
             at = pl.ds(pl.multiple_of((row + a) * self.cols, 16), count * self.cols)
-            part = jnp.dot(
-                self.wide[self.field, at, :], weight[a], preferred_element_type=jnp.float32
-            )
-            total = part if total is None else total + part
-        return total
+            pieces.append(self.wide[self.field, at, :])
+        return jnp.dot(
+            jnp.concatenate(pieces, axis=1), weight[...], preferred_element_type=jnp.float32
+        )
 
     def outer(self, delta, grad, a):
         span = self.rows * self.cols
@@ -338,13 +335,21 @@
     ]
 
 
+def turn_taps(source, target, ch):
+    @pl.loop(0, 9)
+    def _(tap):
+        origin = pl.multiple_of((8 - tap) * ch, ch)
+        at = pl.multiple_of(tap * ch, ch)
+        target[pl.ds(at, ch), :] = source[pl.ds(origin, ch), :].T
+
+
 def main_kernel(plan, size, inputs, filter_one, filter_two, cotangent, *refs):
     input_grad, out_one, out_two = refs[:3]
     wide, edges, lines, got, gathered, corners, halo_send, halo_recv = refs[3:11]
     slope_one, flip_one, flip_two, grad_one, grad_two = refs[11:16]
     scratch = refs[16:]
     rows, cols, ch = size
-    step = 4 if rows % 4 == 0 else 1
+    step = 8 if rows % 8 == 0 else 1
     greet(neighbours() + reduction_peers(plan))
     x, act, delta_two, delta_one = [
         Halo(f, size, wide, edges, lines, got, gathered, corners, halo_send, halo_recv)
@@ -362,14 +367,7 @@
 
     x.send()
     x.shift()
-    for source, target in ((filter_two, flip_two), (filter_one, flip_one)):
-
-        @pl.loop(0, 3)
-        def _(a):
-            for b in range(3):
-                tap = source[2 - a, (2 - b) * ch : (3 - b) * ch, :]
-                target[a, b * ch : (b + 1) * ch, :] = tap.T
-
+    turn_taps(filter_one, flip_one, ch)
     x.receive()
 
     @pl.loop(0, rows // step)
@@ -380,6 +378,7 @@
 
     act.send()
     act.shift()
+    turn_taps(filter_two, flip_two, ch)
     act.receive()
 
     @pl.loop(0, rows // step)
@@ -402,37 +401,23 @@
 
     delta_one.send()
     delta_one.shift()
-    sum_two.step(1)
-    number = 2
     for a in range(3):
         x.outer(delta_one, grad_one, a)
         sum_one.start_part(a)
-        if number < sum_two.steps:
-            sum_two.step(number)
-            number += 1
+    sum_two.step(1)
     delta_one.receive()
-    done = 0
-    pieces = 2 if rows // step % 2 == 0 else 1
-    for piece in range(pieces):
-        sum_one.step(done)
-        done += 1
-        if number < sum_two.steps:
-            sum_two.step(number)
-            number += 1
-        first = piece * (rows // step // pieces)
-
-        @pl.loop(first, first + rows // step // pieces)
-        def _(c):
-            out = delta_one.conv(c * step, step, flip_one)
-            input_grad[block(c * step), :] = out.astype(jnp.bfloat16)
-
-    while done < sum_one.steps or number < sum_two.steps:
-        if done < sum_one.steps:
-            sum_one.step(done)
-            done += 1
-        if number < sum_two.steps:
-            sum_two.step(number)
-            number += 1
+    sum_one.step(0)
+    sum_two.step(2)
+
+    @pl.loop(0, rows // step)
+    def _(c):
+        out = delta_one.conv(c * step, step, flip_one)
+        input_grad[block(c * step), :] = out.astype(jnp.bfloat16)
+
+    for number in range(1, sum_one.steps):
+        sum_one.step(number)
+        if number + 2 < sum_two.steps:
+            sum_two.step(number + 2)
     for one in (x, act, delta_two, delta_one, sum_one, sum_two):
         one.finish()
 
@@ -448,16 +433,15 @@
 
 
 def unpacked(out, plan, shape):
-    value = out[:, :, : plan.rows, :].astype(jnp.float32)
-    return jnp.concatenate([value[0], value[1]], axis=-1).reshape(shape)
+    return out[:, : plan.rows, :].astype(jnp.float32).reshape(shape)
 
 
 def body(mesh, inputs, first_filter, second_filter, cotangent):
     rows, cols, ch = inputs.shape
     plan = Plan(mesh, 3 * ch)
-    if plan.lon < 2 or cols % 16 or rows % 16:
+    if cols % 16 or rows % 16:
         raise ValueError("block size")
-    out = jax.ShapeDtypeStruct((2, PARTS, plan.padded, ch // 2), jnp.bfloat16)
+    out = jax.ShapeDtypeStruct((PARTS, plan.padded, ch), jnp.bfloat16)
     vmem = pl.BlockSpec(memory_space=pltpu.VMEM)
     flat = (rows * cols, ch)
     input_grad, first, second = pl.pallas_call(
@@ -475,8 +459,8 @@
             pltpu.SemaphoreType.DMA((4, 8)),
             pltpu.SemaphoreType.DMA((4, 8)),
             pltpu.VMEM(flat, jnp.float32),
-            pltpu.VMEM((3, 3 * ch, ch), jnp.bfloat16),
-            pltpu.VMEM((3, 3 * ch, ch), jnp.bfloat16),
+            pltpu.VMEM((9 * ch, ch), jnp.bfloat16),
+            pltpu.VMEM((9 * ch, ch), jnp.bfloat16),
             pltpu.VMEM((9 * ch, ch), jnp.float32),
             pltpu.VMEM((9 * ch, ch), jnp.float32),
         ]
@@ -486,8 +470,8 @@
         ),
     )(
         inputs.reshape(flat),
-        first_filter.reshape(3, 3 * ch, ch),
-        second_filter.reshape(3, 3 * ch, ch),
+        first_filter.reshape(9 * ch, ch),
+        second_filter.reshape(9 * ch, ch),
         cotangent.reshape(flat),
     )
     shape = first_filter.shape

time: 85.5 us -> 69.6 us (0.81)
  Pallas kernels: 78.6 us -> 63.3 us
  local copies, waits for them, and re-layouts: 2.9 us -> 0.89 us
  other arithmetic: 3.15 us -> 4.62 us
    pallas_call x1, Pallas kernels: 78.6 us -> 63.3 us  [body(): pl.pallas_call(functools.partial(main_kernel, plan, (rows, cols, ch)), ou...]
    reshape x0 -> x2, other arithmetic: none -> 4.62 us  [unpacked(): return out[:, :plan.rows, :].astype(jnp.float32).reshape(shape)]
    concatenate x2 -> x0, other arithmetic: 3.15 us -> none  [unpacked(): return jnp.concatenate([value[0], value[1]], axis=-1).reshape(shape)]
    slice x1 -> x0, local copies, waits for them, and re-layouts: 2.02 us -> none  [unpacked(): return jnp.concatenate([value[0], value[1]], axis=-1).reshape(shape)]
where the time goes in v3:
time: 69.6 us; the launch traced here: 69.5 us
  Pallas kernels  63.3 us (91%)
  other arithmetic  4.62 us (7%)
  local copies, waits for them, and re-layouts  0.89 us (1%)
    pallas_call x1, Pallas kernels, body(): pl.pallas_call(functools.partial(main_kernel, plan, (rows, cols, ch)), ou...  63.3 us
    reshape x2, other arithmetic, unpacked(): return out[:, :plan.rows, :].astype(jnp.float32).reshape(shape)  4.62 us

profile of v3, /device:TPU:0, one launch (start us, length us, event | category | flops | bytes accessed | tf_op | source)
XLA Modules:
  0.0 69.5 jit_solution(17866743719479639143)
XLA Ops:
  0.6 63.3 %shard_map.67 = (bf16[1536,256]{1,0:T(8,128)(2,1)}, bf16[3,768,256]{2,1,0:T(8,128)(2,1)}, bf16[3,768,256]{2,1,0:T(8,128)(2,1)}) custom-call(bf16[1536,256]{1,0:T(8,128)(2,1)} %bitcast.14, bf16[2304,256]{1,0:T(8,128)(2,1)} %bitcast.11, bf16[2304,256]{1,0:T(8,128)(2,1)} %bitcast.12, bf16[1536,256]{1,0:T(8,128)(2,1)} %bitcast.15), custom_call_target="tpu_custom_call" | custom-call | tf_op jit(solution)/shard_map/pallas_call | solution.py:447
  63.9 0.0 copy-start
  64.0 3.0 %convert.2 = f32[3,3,256,256]{3,2,1,0:T(8,128)} convert(bf16[3,3,256,256]{3,2,1,0:T(8,128)(2,1)} %bitcast.10) | non-fusion elementwise | flops 589824 | bytes 3538944 | tf_op jit(solution)/shard_map/reshape | solution.py:436
  66.9 0.0 copy-done
  66.9 0.0 copy-start.1
  67.0 1.6 %convert.3 = f32[3,3,256,256]{3,2,1,0:T(8,128)} convert(bf16[3,3,256,256]{3,2,1,0:T(8,128)(2,1)S(1)} %bitcast.9) | non-fusion elementwise | flops 589824 | bytes 3538944 | tf_op jit(solution)/shard_map/reshape | solution.py:436
  68.6 0.0 copy-done.1
  68.6 0.9 %copy.8 = bf16[16,96,256]{2,1,0:T(8,128)(2,1)} copy(bf16[16,96,256]{2,1,0:T(8,128)(2,1)S(1)} %bitcast.13) | data formatting | bytes 1572864
Async XLA Ops:
  63.9 3.0 %copy-start = (bf16[3,768,256]{2,1,0:T(8,128)(2,1)S(1)}, bf16[3,768,256]{2,1,0:T(8,128)(2,1)}, u32[]{:S(2)}) copy-start(bf16[3,768,256]{2,1,0:T(8,128)(2,1)} %get-tuple-element.8) | copy-start | bytes 3538948
  66.9 1.6 %copy-start.1 = (bf16[1536,256]{1,0:T(8,128)(2,1)S(1)}, bf16[1536,256]{1,0:T(8,128)(2,1)}, u32[]{:S(2)}) copy-start(bf16[1536,256]{1,0:T(8,128)(2,1)} %get-tuple-element.6) | copy-start | bytes 2359300
